TPU v7x, 32 devices: a whole 2x2x4 slice. The times are simulated.
32 devices in a mesh: dp: 16 (over z, x, core), mp: 2 (over y).
Axes of the slice: x: 2, y: 2, z: 4, core: 2. Of those that a mesh axis runs over, the one named last changes fastest.
Arguments:
- clean: bfloat16 [16, 1024, 1280], P('dp', 'mp'), may hold values from -6 to 6
- noise: bfloat16 [16, 1024, 1280], P('dp', 'mp'), may hold values from -6 to 6
- tsteps: int32 [16], P('dp'), may hold values from 0 to 999
- alpha_tab: float32 [1000], replicated, may hold values from 0.3 to 0.99
- weight_tab: float32 [1000], replicated, may hold values from 0.1 to 3
- norm1_gain: float32 [1280], replicated, may hold values from 0.1 to 1.9
- norm2_gain: float32 [1280], replicated, may hold values from 0.1 to 1.9
- wqkv: bfloat16 [3, 1280, 1280], P(None, 'dp', 'mp'), may hold values from -4 to 4
- wout: bfloat16 [1280, 1280], P('dp', 'mp'), may hold values from -0.625 to 0.625
- wgate: bfloat16 [1280, 5120], P('dp', 'mp'), may hold values from -0.15625 to 0.15625
- wvalue: bfloat16 [1280, 5120], P('dp', 'mp'), may hold values from -0.15625 to 0.15625
- wdown: bfloat16 [5120, 1280], P('mp', 'dp'), may hold values from -0.078125 to 0.078125
Outputs:
- denoised: float32 [16, 1024, 1280], P('dp', 'mp')
- loss: float32 [], replicated
All inputs are finite; a program needn't handle non-finite values.
Results may differ from a plain program's by a relative error of at most 0.02.
Values may be sent and summed in bfloat16 or wider, within the bound.
No kernel may reach another device: no remote copies, remote signals or barrier semaphores. Data moves between devices by JAX's collectives and lax.ppermute only.
A program may use at most 128 MiB of HBM per device.

v0:
```python
import jax
import jax.numpy as jnp
from jax import lax
from jax.sharding import PartitionSpec as P

D = 1280
HEADS = 20
HEAD = 64
L = 1024


def lookup(steps, table):
    match = steps[:, None] == jnp.arange(table.shape[0], dtype=jnp.int32)[None, :]
    return jnp.sum(jnp.where(match, table[None, :], jnp.zeros((), table.dtype)), axis=1)


def layer_norm(values, gain):
    wide = values.astype(jnp.float32)
    center = wide - jnp.mean(wide, axis=-1, keepdims=True)
    spread = jnp.mean(center * center, axis=-1, keepdims=True)
    return (center * lax.rsqrt(spread + 1e-05) * gain).astype(jnp.bfloat16)


def make_adder(flat, piece):
    return jnp.einsum("rn,tnc->trc", flat, piece, preferred_element_type=jnp.float32)


def attend(operands):
    query_one, keys_one, values_one = operands
    rows = query_one.shape[0]
    total = keys_one.shape[0]
    scores = jnp.einsum(
        "qhd,khd->hqk",
        query_one.reshape(rows, HEADS, HEAD),
        keys_one.reshape(total, HEADS, HEAD),
        preferred_element_type=jnp.float32,
    ) * HEAD ** (-0.5)
    probs = jax.nn.softmax(scores, axis=-1).astype(jnp.bfloat16)
    mixed = jnp.einsum(
        "hqk,khd->qhd",
        probs,
        values_one.reshape(total, HEADS, HEAD),
        preferred_element_type=jnp.float32,
    )
    return mixed.astype(jnp.bfloat16).reshape(rows, D)


def shards(
    clean,
    noise,
    tsteps,
    alpha_tab,
    weight_tab,
    norm1_gain,
    norm2_gain,
    wqkv,
    wout,
    wgate,
    wvalue,
    wdown,
):
    samples, local_rows, width = clean.shape
    alpha = lookup(tsteps, alpha_tab)
    sigma = jnp.sqrt(1.0 - alpha * alpha)
    weight = lookup(tsteps, weight_tab)
    noised = (
        alpha[:, None, None] * clean.astype(jnp.float32)
        + sigma[:, None, None] * noise.astype(jnp.float32)
    ).astype(jnp.bfloat16)
    normed1 = layer_norm(noised, norm1_gain)
    full_cols = lax.all_gather(wqkv, "mp", axis=2, tiled=True)
    flat = normed1.reshape(samples * local_rows, width)
    projected = make_adder(flat, lax.all_gather(full_cols, "dp", axis=1, tiled=True)).astype(
        jnp.bfloat16
    )
    query = projected[0].reshape(samples, local_rows, width)
    keys_part = projected[1].reshape(samples, local_rows, width)
    values_part = projected[2].reshape(samples, local_rows, width)
    keys_all, values_all = (
        lax.all_gather(keys_part, "mp", axis=1, tiled=True),
        lax.all_gather(values_part, "mp", axis=1, tiled=True),
    )
    mixed = lax.map(attend, (query, keys_all, values_all))
    mixed_flat = mixed.reshape(samples * local_rows, width)
    out_cols = lax.all_gather(wout, "mp", axis=1, tiled=True)
    part = mixed_flat
    projected_out = jnp.dot(
        part, lax.all_gather(out_cols, "dp", axis=0, tiled=True), preferred_element_type=jnp.float32
    )
    resid = (noised.astype(jnp.float32) + projected_out.reshape(samples, local_rows, width)).astype(
        jnp.bfloat16
    )
    normed2 = layer_norm(resid, norm2_gain)
    ff_in = lax.all_gather(normed2, "mp", axis=1, tiled=True)
    all_rows = ff_in.shape[1]
    ff_flat = ff_in.reshape(samples * all_rows, width)
    part = ff_flat
    gate = jnp.dot(
        part, lax.all_gather(wgate, "dp", axis=0, tiled=True), preferred_element_type=jnp.float32
    )
    value = jnp.dot(
        part, lax.all_gather(wvalue, "dp", axis=0, tiled=True), preferred_element_type=jnp.float32
    )
    hidden = (jax.nn.gelu(gate, approximate=False) * value).astype(jnp.bfloat16)
    block_sum = jnp.dot(
        hidden, lax.all_gather(wdown, "dp", axis=1, tiled=True), preferred_element_type=jnp.float32
    )
    ff_out = lax.psum_scatter(
        block_sum.reshape(samples, all_rows, width).astype(jnp.bfloat16),
        "mp",
        scatter_dimension=1,
        tiled=True,
    ).astype(jnp.float32)
    prediction = resid.astype(jnp.float32) + ff_out
    denoised = (noised.astype(jnp.float32) - sigma[:, None, None] * prediction) / alpha[
        :, None, None
    ]
    error = denoised - clean.astype(jnp.float32)
    local_terms = jnp.sum(weight * jnp.sum(error * error, axis=(1, 2))) / (L * D)
    loss = lax.psum(local_terms, ("dp", "mp"))
    return (denoised, loss)


def solution(mesh):
    in_specs = (
        P("dp", "mp", None),
        P("dp", "mp", None),
        P("dp"),
        P(),
        P(),
        P(),
        P(),
        P(None, "dp", "mp"),
        P("dp", "mp"),
        P("dp", "mp"),
        P("dp", "mp"),
        P("mp", "dp"),
    )
    out_specs = (P("dp", "mp", None), P())
    return jax.shard_map(shards, mesh=mesh, in_specs=in_specs, out_specs=out_specs, check_vma=False)
```

profile of v0, /device:TPU:0, one launch (start us, length us, event | category | flops | bytes accessed | tf_op | source)
XLA Modules:
  0.0 603.2 jit_solution(5153654277553743929)
XLA Ops:
  7.2 12.9 %all_gather.30 = bf16[3,80,1280]{2,1,0:T(8,128)(2,1)} all-gather(bf16[3,80,640]{2,1,0:T(8,128)(2,1)} %param.19), channel_id=1, replica_groups=mesh['dp'=16,'mp'=2] {'mp'}, dimensions={2}, use_global_device_ids=true | all-gather | bytes 921600 | tf_op jit(solution)/shard_map/all_gather | solution.py:71
  20.8 1.4 select_reduce_fusion.1
  23.6 3.0 convert_reduce_fusion
  27.1 76.9 %all-gather.9.cloned.1.call-done = bf16[3,1280,1280]{2,1,0:T(8,128)(2,1)} async-done(((bf16[3,80,1280]{2,1,0:T(8,128)(2,1)}), bf16[3,1280,1280]{2,1,0:T(8,128)(2,1)}) %all-gather.9.cloned.1.call-update) | async-done | bytes 9830416 | tf_op jit(solution)/shard_map/all_gather | solution.py:73
  104.0 9.6 %fusion.49 = bf16[3,512,1280]{2,1,0:T(8,128)(2,1)S(1)} fusion(bf16[3,1280,1280]{2,1,0:T(8,128)(2,1)} %all-gather.9.cloned.1.call-done, bf16[1,512,1280]{2,1,0:T(8,128)(2,1)S(1)} %get-tuple-element.20, f32[1280]{0:T(1024)S(1)} %copy-done.8, f32[512]{0:T(512)S(1)} %add_rsqrt_fusion.1, f32[512]{0:T(512)S(1)} %broadcast_multiply_fusion.1), kind=kOutput, calls=%fused_computation.67 | convolution fusion | flops 5038407680 | bytes 15082496 | tf_op jit(solution)/shard_map/rn,tnc->trc/dot_general | solution.py:25
  113.6 1.8 fusion.113
  115.5 0.7 all-gather.11.cloned.1.call-update
  116.2 5.8 all_gather.34
  122.1 0.5 all-gather.19.cloned.1.call-update
  122.9 1.5 copy.18
  124.3 28.6 %all-gather.13.cloned.1.call-done = bf16[1,1024,1280]{2,1,0:T(8,128)(2,1)} async-done(((bf16[1,512,1280]{2,1,0:T(8,128)(2,1)}), bf16[1,1024,1280]{2,1,0:T(8,128)(2,1)}) %all-gather.13.cloned.1.call-update) | async-done | bytes 2621456 | tf_op jit(solution)/shard_map/all_gather | solution.py:80
  152.9 4.5 copy.19
  157.4 36.1 %all-gather.11.cloned.1.call-done = bf16[1,1024,1280]{2,1,0:T(8,128)(2,1)} async-done(((bf16[1,512,1280]{2,1,0:T(8,128)(2,1)}), bf16[1,1024,1280]{2,1,0:T(8,128)(2,1)}) %all-gather.11.cloned.1.call-update) | async-done | bytes 2621456 | tf_op jit(solution)/shard_map/all_gather | solution.py:81
  193.5 4.4 copy.17
  197.9 19.6 %fusion.114 = (f32[20,512]{1,0:T(8,128)S(1)}, f32[20,512,1024]{2,1,0:T(8,128)}) fusion(bf16[512,20,64]{0,2,1:T(8,128)(2,1)S(1)} %bitcast.42, bf16[1024,20,64]{0,2,1:T(8,128)(2,1)} %bitcast.40), kind=kOutput, calls=%fused_computation.137 | convolution fusion | flops 1373635584 | bytes 45916160 | tf_op jit(solution)/shard_map/while/body/eval_jaxpr/sub | solution.py:38
  217.5 16.5 %fusion.74 = bf16[20,64,512]{2,1,0:T(8,128)(2,1)S(1)} fusion(bf16[1024,20,64]{0,2,1:T(8,128)(2,1)} %bitcast.41, f32[20,512,1024]{2,1,0:T(8,128)} %get-tuple-element.25, f32[20,512]{1,0:T(8,128)S(1)} %get-tuple-element.24), kind=kOutput, calls=%fused_computation.93 | convolution fusion | flops 1363804160 | bytes 45916160 | tf_op jit(solution)/shard_map/while/body/eval_jaxpr/hqk,khd->qhd/dot_general | solution.py:39
  234.0 7.9 %all-gather.15.cloned.1.call-done = bf16[1280,1280]{1,0:T(8,128)(2,1)} async-done(((bf16[80,1280]{1,0:T(8,128)(2,1)}), bf16[1280,1280]{1,0:T(8,128)(2,1)}) %all-gather.15.cloned.1.call-update) | async-done | bytes 3276816 | tf_op jit(solution)/shard_map/all_gather | solution.py:88
  241.9 4.0 convert_reduce_fusion.1
  246.3 0.6 copy-done.2
  246.9 1.5 fusion.63
  248.5 0.7 all-gather.21.cloned.1.call-update
  249.2 0.7 all-gather.23.cloned.1.call-update
  250.0 55.2 %all-gather.19.cloned.1.call-done = bf16[1280,2560]{1,0:T(8,128)(2,1)} async-done(((bf16[80,2560]{1,0:T(8,128)(2,1)}), bf16[1280,2560]{1,0:T(8,128)(2,1)}) %all-gather.19.cloned.1.call-update) | async-done | bytes 6553616 | tf_op jit(solution)/shard_map/all_gather | solution.py:99
  305.2 39.7 %all-gather.17.cloned.1.call-done = bf16[1,1024,1280]{2,1,0:T(8,128)(2,1)} async-done(((bf16[1,512,1280]{2,1,0:T(8,128)(2,1)}), bf16[1,1024,1280]{2,1,0:T(8,128)(2,1)}) %all-gather.17.cloned.1.call-update) | async-done | bytes 2621456 | tf_op jit(solution)/shard_map/all_gather | solution.py:94
  344.9 12.7 %fusion.72 = f32[1024,2560]{1,0:T(8,128)} fusion(bf16[1280,2560]{1,0:T(8,128)(2,1)} %all-gather.19.cloned.1.call-done, bf16[1,1024,1280]{2,1,0:T(8,128)(2,1)} %all-gather.17.cloned.1.call-done), kind=kOutput, calls=%fused_computation.91 | convolution fusion | flops 6710886400 | bytes 19660800 | tf_op jit(solution)/shard_map/dot_general | solution.py:98
  357.6 52.4 %all-gather.21.cloned.1.call-done = bf16[1280,2560]{1,0:T(8,128)(2,1)} async-done(((bf16[80,2560]{1,0:T(8,128)(2,1)}), bf16[1280,2560]{1,0:T(8,128)(2,1)}) %all-gather.21.cloned.1.call-update) | async-done | bytes 6553616 | tf_op jit(solution)/shard_map/all_gather | solution.py:102
  410.1 63.9 %all-gather.23.cloned.1.call-done = bf16[2560,1280]{0,1:T(8,128)(2,1)} async-done(((bf16[2560,80]{0,1:T(8,128)(2,1)}), bf16[2560,1280]{0,1:T(8,128)(2,1)}) %all-gather.23.cloned.1.call-update) | async-done | bytes 6553616 | tf_op jit(solution)/shard_map/all_gather | solution.py:106
  474.0 40.1 %fusion.52 = bf16[1,1024,1280]{2,1,0:T(8,128)(2,1)} fusion(bf16[2560,1280]{0,1:T(8,128)(2,1)} %all-gather.23.cloned.1.call-done, f32[1024,2560]{1,0:T(8,128)} %fusion.72, bf16[1280,2560]{1,0:T(8,128)(2,1)} %all-gather.21.cloned.1.call-done, bf16[1,1024,1280]{2,1,0:T(8,128)(2,1)} %all-gather.17.cloned.1.call-done), kind=kOutput, calls=%fused_computation.72 | convolution fusion | flops 13596098560 | bytes 28835840 | tf_op jit(solution)/shard_map/dot_general | solution.py:105
  514.2 0.7 select_reduce_fusion
  514.8 35.9 %reduce-scatter.2.cloned.1.call-done = bf16[1,512,1280]{2,1,0:T(8,128)(2,1)} async-done(((bf16[1,1024,1280]{2,1,0:T(8,128)(2,1)}), bf16[1,512,1280]{2,1,0:T(8,128)(2,1)}) %reduce-scatter.2.cloned.1.call-update) | async-done | bytes 1310736 | tf_op jit(solution)/shard_map/reduce_scatter | solution.py:108
  550.7 5.4 fusion.67
  557.4 39.3 %psum.7 = f32[]{:T(128)} all-reduce(f32[]{:T(128)S(6)} %div.40), channel_id=1, replica_groups=mesh['dp'=16,'mp'=2] {'dp','mp'}, use_global_device_ids=true, to_apply=%region_10.11 | all-reduce | flops 1 | bytes 8 | tf_op jit(solution)/shard_map/psum | solution.py:120
  (37 shorter events, 1.6 us)
Async XLA Ops:
  7.2 96.8 %copy-start.8 = (f32[1280]{0:T(1024)S(1)}, f32[1280]{0:T(1024)}, u32[]{:S(2)}) copy-start(f32[1280]{0:T(1024)} %param.17) | copy-start | bytes 15364
  7.2 96.8 %all-gather.9.cloned.1.call-start = ((), (), s32[]{:S(2)}) async-start(), calls=%async_computation.1 | async-start | bytes 10444800 | tf_op jit(solution)/shard_map/all_gather | solution.py:73
  20.1 132.8 %all-gather.13.cloned.1.call-start = ((), (), s32[]{:S(2)}) async-start(), calls=%async_computation.3 | async-start | bytes 3932160 | tf_op jit(solution)/shard_map/all_gather | solution.py:80
  26.6 215.2 %copy-start = (bf16[1,512,1280]{2,1,0:T(8,128)(2,1)}, bf16[1,512,1280]{2,1,0:T(8,128)(2,1)S(1)}, u32[]{:S(2)}) copy-start(bf16[1,512,1280]{2,1,0:T(8,128)(2,1)S(1)} %get-tuple-element.20) | copy-start | bytes 3932164
  113.6 2.6 copy-start.5
  115.4 78.1 %all-gather.11.cloned.1.call-start = ((), (), s32[]{:S(2)}) async-start(), calls=%async_computation.2 | async-start | bytes 3932160 | tf_op jit(solution)/shard_map/all_gather | solution.py:81
  116.1 125.7 %all-gather.15.cloned.1.call-start = ((), (), s32[]{:S(2)}) async-start(), calls=%async_computation.4 | async-start | bytes 3481600 | tf_op jit(solution)/shard_map/all_gather | solution.py:88
  122.0 183.1 %all-gather.19.cloned.1.call-start = ((), (), s32[]{:S(2)}) async-start(), calls=%async_computation.6 | async-start | bytes 6963200 | tf_op jit(solution)/shard_map/all_gather | solution.py:99
  122.6 222.3 %all-gather.17.cloned.1.call-start = ((), (), s32[]{:S(2)}) async-start(), calls=%async_computation.5 | async-start | bytes 3932160 | tf_op jit(solution)/shard_map/all_gather | solution.py:94
  124.3 73.6 %copy-start.4 = (bf16[1,512,1280]{1,2,0:T(8,128)(2,1)S(1)}, bf16[1,512,1280]{1,2,0:T(8,128)(2,1)}, u32[]{:S(2)}) copy-start(bf16[1,512,1280]{1,2,0:T(8,128)(2,1)} %copy.18) | copy-start | bytes 3932164
  234.0 12.9 %copy-start.6 = (f32[1280]{0:T(1024)S(1)}, f32[1280]{0:T(1024)}, u32[]{:S(2)}) copy-start(f32[1280]{0:T(1024)} %param.18) | copy-start | bytes 15364
  245.8 1.1 copy-start.2
  248.4 161.7 %all-gather.21.cloned.1.call-start = ((), (), s32[]{:S(2)}) async-start(), calls=%async_computation.7 | async-start | bytes 6963200 | tf_op jit(solution)/shard_map/all_gather | solution.py:102
  249.2 224.8 %all-gather.23.cloned.1.call-start = ((), (), s32[]{:S(2)}) async-start(), calls=%async_computation.8 | async-start | bytes 6963200 | tf_op jit(solution)/shard_map/all_gather | solution.py:106
  249.9 300.8 %reduce-scatter.2.cloned.1.call-start = ((), (), s32[]{:S(2)}) async-start(), calls=%async_computation.9 | async-start | bytes 3932160 | tf_op jit(solution)/shard_map/reduce_scatter | solution.py:108
  474.0 40.2 %copy-start.7 = (f32[1000]{0:T(1024)S(1)}, f32[1000]{0:T(1024)}, u32[]{:S(2)}) copy-start(f32[1000]{0:T(1024)} %param.16) | copy-start | bytes 12004
  474.0 76.7 %copy-start.1 = (bf16[1,512,1280]{2,1,0:T(8,128)(2,1)S(1)}, bf16[1,512,1280]{2,1,0:T(8,128)(2,1)}, u32[]{:S(2)}) copy-start(bf16[1,512,1280]{2,1,0:T(8,128)(2,1)} %copy-done) | copy-start | bytes 3932164
  474.0 76.7 %copy-start.3 = (bf16[1,512,1280]{2,1,0:T(8,128)(2,1)S(1)}, bf16[1,512,1280]{2,1,0:T(8,128)(2,1)}, u32[]{:S(2)}) copy-start(bf16[1,512,1280]{2,1,0:T(8,128)(2,1)} %copy-done.2) | copy-start | bytes 3932164
Sparse Core Ops, SparseCore 0:
  20.3 83.6 all-gather.8
  115.5 37.3 all-gather.12
  154.5 38.9 all-gather.10
  195.6 46.1 all-gather.14
  244.0 61.1 all-gather.18
  307.1 37.7 all-gather.16
  347.2 62.8 all-gather.20
  412.4 61.5 all-gather.22
  514.3 36.3 reduce-scatter.1
where the time goes:
time: 604 us; the launch traced here: 603 us
  waiting for transfers between devices  399 us (66%)
  matrix products  103 us (17%)
  blocking collectives  58 us (10%)
  between operations  17.3 us (3%)
  other arithmetic  12.9 us (2%)
  local copies, waits for them, and re-layouts  12.7 us (2%)
    all_gather x1, waiting for transfers between devices, shards(): lax.all_gather(full_cols, 'dp', axis=1, tiled=True)  76.9 us
    all_gather x1, waiting for transfers between devices, shards(): lax.all_gather(wdown, 'dp', axis=1, tiled=True)  63.9 us
    all_gather x1, waiting for transfers between devices, shards(): lax.all_gather(wgate, 'dp', axis=0, tiled=True)  55.2 us
    all_gather x1, waiting for transfers between devices, shards(): lax.all_gather(wvalue, 'dp', axis=0, tiled=True)  52.4 us
    dot_general x1, matrix products, shards(): jnp.dot(hidden, lax.all_gather(wdown, 'dp', axis=1, tiled=True), preferre...  40.1 us
    all_gather x1, waiting for transfers between devices, shards(): ff_in = lax.all_gather(normed2, 'mp', axis=1, tiled=True)  39.7 us
    psum x1, blocking collectives, shards(): loss = lax.psum(local_terms, ('dp', 'mp'))  39.3 us
    all_gather x1, waiting for transfers between devices, shards(): lax.all_gather(values_part, 'mp', axis=1, tiled=True)  36.1 us
  transfers between devices with their start and end apart: 9, of which 9 were waited for; matrix products, arithmetic and copies ran while one was open for 12% of the time, Pallas kernels for 0%

commit v1 on v0

--- a/solution.py
+++ b/solution.py
@@ -1,12 +1,20 @@
+import functools
+
 import jax
 import jax.numpy as jnp
 from jax import lax
+from jax.experimental import pallas as pl
+from jax.experimental.pallas import tpu as pltpu
 from jax.sharding import PartitionSpec as P
 
-D = 1280
+
 HEADS = 20
-HEAD = 64
-L = 1024
+EPS = 1e-05
+CORES = 2
+SIDE = 2
+BF16 = jnp.bfloat16
+F32 = jnp.float32
+VMEM_LIMIT = 24 * 1024 * 1024
 
 
 def lookup(steps, table):
@@ -15,10 +23,378 @@
 
 
 def layer_norm(values, gain):
-    wide = values.astype(jnp.float32)
+    wide = values.astype(F32)
     center = wide - jnp.mean(wide, axis=-1, keepdims=True)
     spread = jnp.mean(center * center, axis=-1, keepdims=True)
-    return (center * lax.rsqrt(spread + 1e-05) * gain).astype(jnp.bfloat16)
+    return (center * lax.rsqrt(spread + EPS) * gain).astype(BF16)
+
+
+def dot(a, b):
+    return jnp.dot(a, b, preferred_element_type=F32)
+
+
+def dot_nt(a, b):
+    return lax.dot_general(a, b, (((1,), (1,)), ((), ())), preferred_element_type=F32)
+
+
+def hbm_spec():
+    return pl.BlockSpec(memory_space=pltpu.HBM)
+
+
+def vmem_spec():
+    return pl.BlockSpec(memory_space=pltpu.VMEM)
+
+
+def smem_spec():
+    return pl.BlockSpec(memory_space=pltpu.SMEM)
+
+
+def call(body, outs, in_specs, scratch, flops, nbytes, trans=0, out_specs=None):
+    return pl.pallas_call(
+        body,
+        out_shape=outs,
+        in_specs=in_specs,
+        out_specs=out_specs if out_specs is not None else [vmem_spec() for _ in outs],
+        scratch_shapes=scratch,
+        compiler_params=pltpu.CompilerParams(vmem_limit_bytes=VMEM_LIMIT),
+        cost_estimate=pl.CostEstimate(flops=flops, bytes_accessed=nbytes, transcendentals=trans),
+    )
+
+
+def piece_base(place, index, lines, rows):
+    z, x = place[0], place[1]
+    base = ((z ^ (index % lines)) * SIDE + (x ^ (index // lines))) * rows
+    return pl.multiple_of(base, rows)
+
+
+def attend_heads(q, k_ref, v_ref, pair, lane_low):
+    k2 = k_ref[pair]
+    v2 = v_ref[pair]
+    halves = []
+    for first in (True, False):
+        keep = lane_low if first else jnp.logical_not(lane_low)
+        qh = jnp.where(keep, q, jnp.zeros_like(q))
+        s = dot_nt(qh, k2)
+        m = jnp.max(s, axis=-1, keepdims=True)
+        e = jnp.exp(s - m)
+        total = jnp.sum(e, axis=-1, keepdims=True)
+        o = dot(e.astype(BF16), v2)
+        halves.append(o * (1.0 / total))
+    return jnp.where(lane_low, halves[0], halves[1]).astype(BF16)
+
+
+def attention_loop(q_ref, q_base, rows, k_ref, v_ref, out_ref, block):
+    pairs = k_ref.shape[0]
+    lane = lax.broadcasted_iota(jnp.int32, (block, 2 * HEAD_LANES), 1)
+    lane_low = lane < HEAD_LANES
+
+    def step(pair, carry):
+        for t in range(rows // block):
+            q = q_ref[pair, pl.ds(q_base + t * block, block), :]
+            mixed = attend_heads(q, k_ref, v_ref, pair, lane_low)
+            out_ref[pair, pl.ds(t * block, block), :] = mixed
+        return carry
+
+    lax.fori_loop(0, pairs, step, 0)
+
+
+HEAD_LANES = 64
+
+
+def qkv_body(scale, lines, place, n_own, n_peer, *refs):
+    q_own, q_peer, k_out, v_out, w, sems = refs[4:]
+    rows = refs[0].shape[1]
+    copies = []
+    for number, ref in enumerate(refs[:4]):
+        slot = (place[2] ^ (number // 2)) * 2 + number % 2
+        for index in range(ref.shape[0]):
+            base = pl.ds(piece_base(place, index, lines, rows), rows)
+            copies.append(pltpu.make_async_copy(ref.at[index], w.at[slot, base, :], sems.at[number // 2]))
+    for cp in copies:
+        cp.start()
+    for cp in copies:
+        cp.wait()
+    half = n_own.shape[0]
+    block = 256
+    pairs = k_out.shape[0]
+    for which, src in enumerate((n_own, n_peer)):
+        for t in range(half // block):
+            a = src[t * block : (t + 1) * block, :]
+            lo = t * block
+            for mat in range(3):
+                r = dot(a, w[mat]).astype(BF16)
+                if mat == 0:
+                    r = r * jnp.asarray(scale, BF16)
+                for p in range(pairs):
+                    col = r[:, p * 128 : (p + 1) * 128]
+                    if mat == 0:
+                        (q_own, q_peer)[which][p, lo : lo + block, :] = col
+                    else:
+                        at = which * half + lo
+                        (k_out, v_out)[mat - 1][p, at : at + block, :] = col
+
+
+def attn_body(q_ref, k_ref, v_ref, mixed_ref):
+    attention_loop(q_ref, 0, q_ref.shape[1], k_ref, v_ref, mixed_ref, 256)
+
+
+def wout_body(lines, place, gain, noised, m_own, m_peer, packed, second, y_own, y_partner, resid_ref, n2_ref, w, sems):
+    rows = packed.shape[1]
+    c = place[2]
+
+    def run(sources, act):
+        for index in range(packed.shape[0]):
+            base = pl.ds(piece_base(place, index, lines, rows), rows)
+            for slot, ref in enumerate(sources):
+                act(pltpu.make_async_copy(ref.at[index], w.at[slot, base, :], sems.at[slot]))
+
+    for act in (lambda cp: cp.start(), lambda cp: cp.wait()):
+
+        @pl.when(c == 1)
+        def _():
+            run((packed, y_own), act)
+
+        @pl.when(c == 0)
+        def _():
+            run((second, y_partner), act)
+
+    y = place[3]
+    pairs = m_own.shape[0]
+    width = pairs * 128
+    block = 256
+    own0 = pl.multiple_of(y * width, width)
+    peer0 = pl.multiple_of((1 - y) * width, width)
+    for t in range(noised.shape[0] // block):
+        sl = slice(t * block, (t + 1) * block)
+        a_own = jnp.concatenate([m_own[p, sl, :] for p in range(pairs)], axis=-1)
+        a_peer = jnp.concatenate([m_peer[p, sl, :] for p in range(pairs)], axis=-1)
+        outs = []
+        for h in range(2):
+            outs.append(dot(a_own, w[h, pl.ds(own0, width), :]) + dot(a_peer, w[h, pl.ds(peer0, width), :]))
+        first = jnp.where(y == 0, outs[0], outs[1])
+        second = jnp.where(y == 0, outs[1], outs[0])
+        out = jnp.concatenate([first, second], axis=-1)
+        r = (noised[sl, :].astype(F32) + out).astype(BF16)
+        resid_ref[sl, :] = r
+        n2_ref[sl, :] = layer_norm(r, gain[...])
+
+
+def ff_body(has_acc, groups, lines, place, x_ref, *refs):
+    half = len(groups)
+    stacks, rest = (refs[:half], refs[half : 2 * half]), refs[2 * half :]
+    acc_in = None
+    if has_acc:
+        acc_in, rest = rest[0], rest[1:]
+    *outs, w, sems = rest
+    acc = outs.pop() if len(outs) == 2 else outs[0]
+    rows = refs[0].shape[2]
+    sub = w.shape[-1]
+    n_sub = refs[0].shape[-1] // sub
+
+    def each(c_flip, s, act):
+        slot = c_flip * n_sub + s
+        cols = pl.ds(pl.multiple_of(s * sub, sub), sub)
+        for group, ref in zip(groups, stacks[c_flip]):
+            for k, index in enumerate(group):
+                base = pl.ds(piece_base(place, index, lines, rows), rows)
+                act(pltpu.make_async_copy(ref.at[k, :, :, cols], w.at[slot, :, base, :], sems.at[slot]))
+
+    for s in range(n_sub):
+        each(0, s, lambda cp: cp.start())
+
+    def product(slot):
+        x = x_ref[...]
+        gate = dot(x, w[slot, 0])
+        value = dot(x, w[slot, 1])
+        hidden = (0.5 * gate * (1.0 + lax.erf(gate * (0.5**0.5))) * value).astype(BF16)
+        return dot_nt(hidden, w[slot, 2])
+
+    if has_acc:
+        acc[...] = acc_in[...]
+    else:
+        acc[...] = jnp.zeros_like(acc)
+    for c_flip in range(CORES):
+
+        def step(s, carry):
+            if c_flip == 0:
+                each(1, s, lambda cp: cp.start())
+            each(c_flip, s, lambda cp: cp.wait())
+            acc[...] += product(c_flip * n_sub + s)
+            return carry
+
+        lax.fori_loop(0, n_sub, step, 0)
+    if outs and outs[0] is not acc:
+        outs[0][...] = acc[...].astype(outs[0].dtype)
+
+
+def fast_shards(dp, chunks, clean, noise, tsteps, alpha_tab, weight_tab, gain1, gain2, wqkv, wout, wgate, wvalue, wdown):
+    _, rows, width = clean.shape
+    heads_width = wout.shape[1]
+    pairs = heads_width // 128
+    lines = dp // (SIDE * CORES)
+    me = lax.axis_index("dp")
+    y = lax.axis_index("mp")
+    c = me % CORES
+    x = (me // CORES) % SIDE
+    z = me // (CORES * SIDE)
+    place = jnp.stack([z, x, c, y]).astype(jnp.int32)
+    gain_row = gain2.reshape(1, width)
+
+    def flip(value, bits):
+        return lax.ppermute(value, "dp", [(i, i ^ bits) for i in range(dp)])
+
+    def flip_y(value):
+        return lax.ppermute(value, "mp", [(0, 1), (1, 0)])
+
+    CORE, XBIT, ZUNIT = 1, CORES, CORES * SIDE
+
+    b0 = jnp.concatenate([wqkv, wout[None]], axis=0)
+    keep0 = lax.dynamic_slice_in_dim(b0, 2 * c, 2, 0)
+    give0 = lax.dynamic_slice_in_dim(b0, 2 * (1 - c), 2, 0)
+    first = c == 0
+
+    def by_core(keep, recv):
+        return jnp.concatenate([jnp.where(first, keep, recv), jnp.where(first, recv, keep)], axis=1)
+
+    own0 = by_core(keep0, flip(give0, CORE))
+
+    alpha = lookup(tsteps, alpha_tab)
+    sigma = jnp.sqrt(1.0 - alpha * alpha)
+    weight = lookup(tsteps, weight_tab)
+    noised = (alpha[0] * clean[0].astype(F32) + sigma[0] * noise[0].astype(F32)).astype(BF16)
+    n1 = layer_norm(noised, gain1)
+    n1_peer = flip_y(n1)
+
+    ffw = jnp.stack([wgate, wvalue, wdown.T])
+    hidden_half = ffw.shape[2] // CORES
+    keep_f = lax.dynamic_slice_in_dim(ffw, c * hidden_half, hidden_half, 2)
+    give_f = lax.dynamic_slice_in_dim(ffw, (1 - c) * hidden_half, hidden_half, 2)
+    recv_f = flip(give_f, CORE)
+
+    def gather(own, late_by_z):
+        zs, xs = [own], []
+        for k in range(1, lines):
+            top = 1 << (k.bit_length() - 1)
+            if k == top:
+                zs.append(flip(own, ZUNIT * k))
+            else:
+                zs.append(flip(zs[top], ZUNIT * (k - top)))
+        for k in range(lines):
+            top = 1 << max(k.bit_length() - 1, 0)
+            if late_by_z and k == lines - 1 and k != top:
+                xs.append(flip(xs[top], ZUNIT * (k - top)))
+            else:
+                xs.append(flip(zs[k], XBIT))
+        return zs, xs
+
+    def swap_packed(parts):
+        packed = jnp.stack(parts)
+        return packed, flip(packed, CORE)
+
+    zs0, xs0 = gather(own0, False)
+    mats = [swap_packed([p[m] for p in zs0 + xs0]) for m in range(2)]
+    packed0, second0 = mats[1]
+
+    half_shape = jax.ShapeDtypeStruct((pairs, rows, 128), BF16)
+    full_shape = jax.ShapeDtypeStruct((pairs, 2 * rows, 128), BF16)
+    wbytes = 4 * width * heads_width * 2
+    scale = HEAD_LANES ** (-0.5)
+    q_own, q_peer, k_all, v_all = call(
+        functools.partial(qkv_body, scale, lines),
+        [half_shape, half_shape, full_shape, full_shape],
+        [smem_spec(), vmem_spec(), vmem_spec()] + [hbm_spec()] * 4,
+        [
+            pltpu.VMEM((4, width, heads_width), BF16),
+            pltpu.SemaphoreType.DMA((2,)),
+        ],
+        8 * 10**9,
+        wbytes + 8 * rows * width,
+    )(place, n1, n1_peer, mats[0][0], packed0, mats[0][1], second0)
+
+    def attend(q):
+        return call(
+            attn_body, [half_shape], [vmem_spec()] * 3, [], 12 * 10**9, 8 * rows * width
+        )(q, k_all, v_all)[0]
+
+    mixed_peer = attend(q_peer)
+    m_recv = flip_y(mixed_peer)
+    mixed_own = attend(q_own)
+
+    y_own = lax.ppermute(
+        packed0, ("dp", "mp"), [(2 * i + j, 2 * i + 1 - j) for i in range(1, dp, CORES) for j in range(2)]
+    )
+    y_partner = lax.ppermute(y_own, "dp", [(i, i - 1) for i in range(1, dp, CORES)])
+    resid, n2 = call(
+        functools.partial(wout_body, lines),
+        [jax.ShapeDtypeStruct((rows, width), BF16)] * 2,
+        [smem_spec()] + [vmem_spec()] * 4 + [hbm_spec()] * 4,
+        [pltpu.VMEM((2, width, heads_width), BF16), pltpu.SemaphoreType.DMA((2,))],
+        4 * 10**9,
+        wbytes,
+    )(place, gain_row, noised, mixed_own, m_recv, packed0, second0, y_own, y_partner)
+    n2_peer = flip_y(n2)
+
+    def ff(tokens, groups, stacks, hc, sub, acc, out_dtype):
+        n_sub = hc // sub
+        t = tokens.shape[0]
+        args = [place, tokens, *stacks]
+        specs = [smem_spec(), vmem_spec()] + [hbm_spec()] * len(stacks)
+        if acc is not None:
+            args.append(acc)
+            specs.append(vmem_spec())
+        return call(
+            functools.partial(ff_body, acc is not None, groups, lines),
+            [jax.ShapeDtypeStruct((t, width), out_dtype)],
+            specs,
+            ([pltpu.VMEM((t, width), F32)] if out_dtype != F32 else [])
+            + [
+                pltpu.VMEM((CORES * n_sub, 3, width, sub), BF16),
+                pltpu.SemaphoreType.DMA((CORES * n_sub,)),
+            ],
+            2 * t * width * hc * 2 * 3,
+            3 * width * hc * 4,
+        )(*args)[0]
+
+    peer_acc = own_acc = None
+    start = 0
+    for index, hc in enumerate(chunks):
+        sub = 256 if hc % 256 == 0 else 128
+        part = slice(start, start + hc)
+        zs, xs = gather(by_core(keep_f[:, :, part], recv_f[:, :, part]), index > 0)
+        pieces = zs + xs
+        groups = [tuple(range(lines)), tuple(range(lines, 2 * lines, 2))]
+        groups += [(n,) for n in range(lines + 1, 2 * lines, 2)]
+        stacks = []
+        for group in groups:
+            if len(group) > 1:
+                stacks.append(swap_packed([pieces[n] for n in group]))
+            else:
+                piece = pieces[group[0]]
+                stacks.append((piece[None], flip(piece, CORE)[None]))
+        stacks = [pair[n] for n in range(2) for pair in stacks]
+        last = index == len(chunks) - 1
+        peer_acc = ff(n2_peer, groups, stacks, hc, sub, peer_acc, BF16 if last else F32)
+        own_acc = ff(n2, groups, stacks, hc, sub, own_acc, F32)
+        start += hc
+    recv = flip_y(peer_acc)
+
+    ratio = sigma[0] / alpha[0]
+    base = noised.astype(F32) / alpha[0] - ratio * (resid.astype(F32) + own_acc)
+    base = lax.optimization_barrier(base)
+    denoised = base - ratio * recv.astype(F32)
+    error = denoised - clean[0].astype(F32)
+    total = jnp.sum(error * error) * weight[0] / (2 * rows * width)
+
+    term = jnp.full((8, 128), total, F32)
+    term = term + flip(term, CORE)
+    plane = [term, flip(term, XBIT), flip_y(term)]
+    corner = lax.ppermute(
+        term, ("dp", "mp"), [(2 * i + j, 2 * (i ^ XBIT) + (1 - j)) for i in range(dp) for j in range(2)]
+    )
+    term = (plane[0] + plane[1]) + (plane[2] + corner)
+    line = [term] + [flip(term, ZUNIT * k) for k in range(1, lines)]
+    loss = functools.reduce(jnp.add, line)[0, 0]
+    return denoised[None], loss
 
 
 def make_adder(flat, piece):
@@ -31,21 +407,21 @@
     total = keys_one.shape[0]
     scores = jnp.einsum(
         "qhd,khd->hqk",
-        query_one.reshape(rows, HEADS, HEAD),
-        keys_one.reshape(total, HEADS, HEAD),
+        query_one.reshape(rows, HEADS, -1),
+        keys_one.reshape(total, HEADS, -1),
         preferred_element_type=jnp.float32,
-    ) * HEAD ** (-0.5)
+    ) * (query_one.shape[1] // HEADS) ** (-0.5)
     probs = jax.nn.softmax(scores, axis=-1).astype(jnp.bfloat16)
     mixed = jnp.einsum(
         "hqk,khd->qhd",
         probs,
-        values_one.reshape(total, HEADS, HEAD),
+        values_one.reshape(total, HEADS, -1),
         preferred_element_type=jnp.float32,
     )
-    return mixed.astype(jnp.bfloat16).reshape(rows, D)
-
-
-def shards(
+    return mixed.astype(jnp.bfloat16).reshape(query_one.shape)
+
+
+def plain_shards(
     clean,
     noise,
     tsteps,
@@ -116,25 +492,42 @@
         :, None, None
     ]
     error = denoised - clean.astype(jnp.float32)
-    local_terms = jnp.sum(weight * jnp.sum(error * error, axis=(1, 2))) / (L * D)
+    local_terms = jnp.sum(weight * jnp.sum(error * error, axis=(1, 2))) / (all_rows * width)
     loss = lax.psum(local_terms, ("dp", "mp"))
     return (denoised, loss)
 
 
 def solution(mesh):
-    in_specs = (
-        P("dp", "mp", None),
-        P("dp", "mp", None),
-        P("dp"),
-        P(),
-        P(),
-        P(),
-        P(),
-        P(None, "dp", "mp"),
-        P("dp", "mp"),
-        P("dp", "mp"),
-        P("dp", "mp"),
-        P("mp", "dp"),
-    )
+    dp, mp = mesh.shape["dp"], mesh.shape["mp"]
+    spec_w = P("dp", "mp")
+    in_specs = (P("dp", "mp", None), P("dp", "mp", None), P("dp"), P(), P(), P(), P())
+    in_specs += (P(None, "dp", "mp"), spec_w, spec_w, spec_w, P("mp", "dp"))
     out_specs = (P("dp", "mp", None), P())
-    return jax.shard_map(shards, mesh=mesh, in_specs=in_specs, out_specs=out_specs, check_vma=False)
+    lines = dp // (SIDE * CORES)
+
+    def run(*args):
+        clean, wgate = args[0], args[9]
+        hidden = wgate.shape[1] // (mp * CORES)
+        width = clean.shape[2]
+        fits = (
+            mp == 2
+            and clean.shape[0] == dp
+            and lines * SIDE * CORES == dp
+            and lines & (lines - 1) == 0
+            and width == HEADS * HEAD_LANES
+            and (width // mp) % 128 == 0
+            and hidden % 256 == 0
+            and (clean.shape[1] // mp) % 256 == 0
+        )
+        if fits:
+            first = hidden * 2 // 5 // 256 * 256
+
+            def body(*shards):
+                return fast_shards(dp, (first, hidden - first), *shards)
+
+        else:
+            body = plain_shards
+        step = jax.shard_map(body, mesh=mesh, in_specs=in_specs, out_specs=out_specs, check_vma=False)
+        return step(*args)
+
+    return run

time: 604 us -> 308 us (0.51)
  waiting for transfers between devices: 399 us -> 146 us
  matrix products: 103 us -> 0 us
  Pallas kernels: 0 us -> 76 us
  blocking collectives: 58 us -> 0 us
  starting transfers between devices: 0.54 us -> 40.1 us
  between operations: 17.3 us -> 5.04 us
  other arithmetic: 12.9 us -> 22.3 us
    all_gather x8 -> x0, waiting for transfers between devices: 361 us -> none  [the longest x1 76.9 us: shards(): lax.all_gather(full_cols, 'dp', axis=1, tiled=True)]
    ppermute x0 -> x46, waiting for transfers between devices: none -> 146 us  [the longest x38 125 us: flip(): return lax.ppermute(value, 'dp', [(i, i ^ bits) for i in range(dp)])]
    dot_general x5 -> x0, matrix products: 82.9 us -> none  [the longest x1 40.1 us: shards(): jnp.dot(hidden, lax.all_gather(wdown, 'dp', axis=1, tiled=True), preferre...]
    pallas_call x0 -> x8, Pallas kernels: none -> 76 us  [the longest x4 37.3 us: ff(): call(functools.partial(ff_body, acc is not None, groups, lines), [jax.Sha...]
    ppermute x0 -> x46, starting transfers between devices: none -> 40.1 us  [the longest x38 32.3 us: flip(): return lax.ppermute(value, 'dp', [(i, i ^ bits) for i in range(dp)])]
    psum x1 -> x0, blocking collectives: 39.3 us -> none  [shards(): loss = lax.psum(local_terms, ('dp', 'mp'))]
    reduce_scatter x1 -> x0, waiting for transfers between devices: 35.9 us -> none  [shards(): lax.psum_scatter(block_sum.reshape(samples, all_rows, width).astype(jnp.b...]
    sub x1 -> x0, matrix products: 19.6 us -> none  [attend(): probs = jax.nn.softmax(scores, axis=-1).astype(jnp.bfloat16)]
  transfers between devices with their start and end apart: 9 -> 46, of which waited for: 9 -> 19; matrix products, arithmetic and copies ran while one was open for 12% -> 8% of each run, Pallas kernels for 0% -> 21%
where the time goes in v1:
time: 308 us; the launch traced here: 307 us
  waiting for transfers between devices  146 us (47%)
  Pallas kernels  76 us (25%)
  starting transfers between devices  40.1 us (13%)
  other arithmetic  22.3 us (7%)
  local copies, waits for them, and re-layouts  17.6 us (6%)
  between operations  5.04 us (2%)
    ppermute x38, waiting for transfers between devices, flip(): return lax.ppermute(value, 'dp', [(i, i ^ bits) for i in range(dp)])  125 us
    pallas_call x4, Pallas kernels, ff(): call(functools.partial(ff_body, acc is not None, groups, lines), [jax.Sha...  37.3 us
    ppermute x38, starting transfers between devices, flip(): return lax.ppermute(value, 'dp', [(i, i ^ bits) for i in range(dp)])  32.3 us
    pallas_call x2, Pallas kernels, attend(): call(attn_body, [half_shape], [vmem_spec()] * 3, [], 12 * 10 ** 9, 8 * ro...  20.2 us
    ppermute x5, waiting for transfers between devices, flip_y(): return lax.ppermute(value, 'mp', [(0, 1), (1, 0)])  19 us
    unnamed x64, local copies, waits for them, and re-layouts  15.3 us
    pallas_call x1, Pallas kernels, fast_shards(): call(functools.partial(qkv_body, scale, lines), [half_shape, half_shape,...  10.7 us
    pallas_call x1, Pallas kernels, fast_shards(): call(functools.partial(wout_body, lines), [jax.ShapeDtypeStruct((rows, wi...  7.8 us
  transfers between devices with their start and end apart: 46, of which 19 were waited for; matrix products, arithmetic and copies ran while one was open for 8% of the time, Pallas kernels for 21%

profile of v1, /device:TPU:0, one launch (start us, length us, event | category | flops | bytes accessed | tf_op | source)
XLA Modules:
  0.0 306.8 jit_solution(3716863286895580145)
XLA Ops:
  0.6 1.7 fusion.11
  8.0 2.6 convert_reduce_fusion
  10.9 3.1 %collective-permute-start.2 = (bf16[2,160,640]{2,1,0:T(8,128)(2,1)S(1)}, bf16[2,160,640]{2,1,0:T(8,128)(2,1)S(1)}, u32[]{:S(2)}, u32[]{:S(2)}) collective-permute-start(bf16[2,160,640]{2,1,0:T(8,128)(2,1)S(1)} %pad_maximum_fusion.6), channel_id=1, source_target_pairs={{0,8},{2,10},{4,12},{6,14},{8,0},{10,2},{12,4},{14,6},{16,24},{18,... | collective-permute-start | bytes 1228808 | tf_op jit(solution)/shard_map/ppermute | solution.py:244
  13.9 2.6 collective-permute-start.3
  19.4 15.4 %collective-permute-done.3 = bf16[2,160,640]{2,1,0:T(8,128)(2,1)S(1)} collective-permute-done((bf16[2,160,640]{2,1,0:T(8,128)(2,1)S(1)}, bf16[2,160,640]{2,1,0:T(8,128)(2,1)S(1)}, u32[]{:S(2)}, u32[]{:S(2)}) %collective-permute-start.3) | collective-permute-done | bytes 409632 | tf_op jit(solution)/shard_map/ppermute | solution.py:244
  38.8 5.1 %collective-permute-done.4 = bf16[2,160,640]{2,1,0:T(8,128)(2,1)S(1)} collective-permute-done((bf16[2,160,640]{2,1,0:T(8,128)(2,1)S(1)}, bf16[2,160,640]{2,1,0:T(8,128)(2,1)S(1)}, u32[]{:S(2)}, u32[]{:S(2)}) %collective-permute-start.4) | collective-permute-done | bytes 409632 | tf_op jit(solution)/shard_map/ppermute | solution.py:244
  47.0 9.3 %collective-permute-done.6 = bf16[2,160,640]{2,1,0:T(8,128)(2,1)S(1)} collective-permute-done((bf16[2,160,640]{2,1,0:T(8,128)(2,1)S(1)}, bf16[2,160,640]{2,1,0:T(8,128)(2,1)S(1)}, u32[]{:S(2)}, u32[]{:S(2)}) %collective-permute-start.6) | collective-permute-done | bytes 409632 | tf_op jit(solution)/shard_map/ppermute | solution.py:244
  57.9 5.1 %collective-permute-done.8 = bf16[2,160,640]{2,1,0:T(8,128)(2,1)S(1)} collective-permute-done((bf16[2,160,640]{2,1,0:T(8,128)(2,1)S(1)}, bf16[2,160,640]{2,1,0:T(8,128)(2,1)S(1)}, u32[]{:S(2)}, u32[]{:S(2)}) %collective-permute-start.8) | collective-permute-done | bytes 409632 | tf_op jit(solution)/shard_map/ppermute | solution.py:244
  68.4 2.4 collective-permute-start.27
  71.1 21.7 %collective-permute-done.27 = bf16[3,160,512]{2,1,0:T(8,128)(2,1)} collective-permute-done((bf16[3,160,512]{2,1,0:T(8,128)(2,1)}, bf16[3,160,512]{2,1,0:T(8,128)(2,1)}, u32[]{:S(2)}, u32[]{:S(2)}) %collective-permute-start.27) | collective-permute-done | bytes 491552 | tf_op jit(solution)/shard_map/ppermute | solution.py:244
  95.7 10.4 %collective-permute-done.29 = bf16[3,160,512]{2,1,0:T(8,128)(2,1)S(1)} collective-permute-done((bf16[3,160,512]{2,1,0:T(8,128)(2,1)}, bf16[3,160,512]{2,1,0:T(8,128)(2,1)S(1)}, u32[]{:S(2)}, u32[]{:S(2)}) %collective-permute-start.29) | collective-permute-done | bytes 491552 | tf_op jit(solution)/shard_map/ppermute | solution.py:244
  107.6 2.0 collective-permute-start.28
  110.6 10.7 %shard_map.131 = (bf16[5,512,128]{2,1,0:T(8,128)(2,1)S(1)}, bf16[5,512,128]{2,1,0:T(8,128)(2,1)S(1)}, bf16[5,1024,128]{2,1,0:T(8,128)(2,1)S(1)}, bf16[5,1024,128]{2,1,0:T(8,128)(2,1)S(1)}) custom-call(s32[4]{0:T(128)S(1)} %pad_add_fusion.place, bf16[512,1280]{1,0:T(8,128)(2,1)S(1)} %fusion.4.n_own, bf16[512,1280]{1,0:T(8,128)(2,1)} %collective-permute-done.n_peer, ...), custom_call_target="tpu_custom_call" | custom-call | flops 8000000000 | bytes 11796480 | tf_op jit(solution)/shard_map/pallas_call | solution.py:302
  121.3 8.0 %collective-permute-done.16 = bf16[3,160,768]{2,1,0:T(8,128)(2,1)S(1)} collective-permute-done((bf16[3,160,768]{2,1,0:T(8,128)(2,1)S(1)}, bf16[3,160,768]{2,1,0:T(8,128)(2,1)S(1)}, u32[]{:S(2)}, u32[]{:S(2)}) %collective-permute-start.16) | collective-permute-done | bytes 737312 | tf_op jit(solution)/shard_map/ppermute | solution.py:244
  129.8 11.4 %collective-permute-done.15 = bf16[3,160,768]{2,1,0:T(8,128)(2,1)S(1)} collective-permute-done((bf16[3,160,768]{2,1,0:T(8,128)(2,1)S(1)}, bf16[3,160,768]{2,1,0:T(8,128)(2,1)S(1)}, u32[]{:S(2)}, u32[]{:S(2)}) %collective-permute-start.15) | collective-permute-done | bytes 737312 | tf_op jit(solution)/shard_map/ppermute | solution.py:244
  142.7 9.0 %collective-permute-done.28 = bf16[3,160,512]{2,1,0:T(8,128)(2,1)S(1)} collective-permute-done((bf16[3,160,512]{2,1,0:T(8,128)(2,1)}, bf16[3,160,512]{2,1,0:T(8,128)(2,1)S(1)}, u32[]{:S(2)}, u32[]{:S(2)}) %collective-permute-start.28) | collective-permute-done | bytes 491552 | tf_op jit(solution)/shard_map/ppermute | solution.py:244
  153.2 10.1 %shard_map.133 = bf16[5,512,128]{2,1,0:T(8,128)(2,1)S(1)} custom-call(bf16[5,512,128]{2,1,0:T(8,128)(2,1)S(1)} %get-tuple-element.11.q_ref, bf16[5,1024,128]{2,1,0:T(8,128)(2,1)S(1)} %get-tuple-element.9.k_ref, bf16[5,1024,128]{2,1,0:T(8,128)(2,1)S(1)} %get-tuple-element.10.v_ref), custom_call_target="tpu_custom_call" | custom-call | flops 12000000000 | bytes 5242880 | tf_op jit(solution)/shard_map/pallas_call | solution.py:315
  168.7 1.8 pad_maximum_fusion.refs_0_
  170.5 8.9 %collective-permute-done.32 = bf16[3,160,512]{2,1,0:T(8,128)(2,1)S(1)} collective-permute-done((bf16[3,160,512]{2,1,0:T(8,128)(2,1)S(1)}, bf16[3,160,512]{2,1,0:T(8,128)(2,1)S(1)}, u32[]{:S(2)}, u32[]{:S(2)}) %collective-permute-start.32) | collective-permute-done | bytes 491552 | tf_op jit(solution)/shard_map/ppermute | solution.py:244
  181.3 10.1 %shard_map.132.m_own = bf16[5,512,128]{2,1,0:T(8,128)(2,1)S(1)} custom-call(bf16[5,512,128]{2,1,0:T(8,128)(2,1)S(1)} %get-tuple-element.8.q_ref, bf16[5,1024,128]{2,1,0:T(8,128)(2,1)S(1)} %get-tuple-element.9.k_ref, bf16[5,1024,128]{2,1,0:T(8,128)(2,1)S(1)} %get-tuple-element.10.v_ref), custom_call_target="tpu_custom_call" | custom-call | flops 12000000000 | bytes 5242880 | tf_op jit(solution)/shard_map/pallas_call | solution.py:315
  192.0 7.8 %shard_map.134 = (bf16[512,1280]{1,0:T(8,128)(2,1)S(1)}, bf16[512,1280]{1,0:T(8,128)(2,1)}) custom-call(s32[4]{0:T(128)S(1)} %pad_add_fusion.place, f32[1,1280]{1,0:T(1,128)S(1)} %reshape.41.gain, bf16[512,1280]{1,0:T(8,128)(2,1)S(1)} %get-tuple-element.15.noised, bf16[5,512,128]{2,1,0:T(8,128)(2,1)S(1)} %shard_map.132.m_own, ...), custom_call_target="tpu_custom_call" | custom-call | flops 4000000000 | bytes 6553600 | tf_op jit(solution)/shard_map/pallas_call | solution.py:327
  202.7 2.4 pad_maximum_fusion.2.refs_1_
  207.3 14.2 %collective-permute-done.21 = bf16[3,160,768]{2,1,0:T(8,128)(2,1)} collective-permute-done((bf16[3,160,768]{2,1,0:T(8,128)(2,1)}, bf16[3,160,768]{2,1,0:T(8,128)(2,1)}, u32[]{:S(2)}, u32[]{:S(2)}) %collective-permute-start.21) | collective-permute-done | bytes 737312 | tf_op jit(solution)/shard_map/ppermute | solution.py:244
  228.6 7.6 %shard_map.135.refs_8_ = f32[512,1280]{1,0:T(8,128)S(1)} custom-call(s32[4]{0:T(128)S(1)} %pad_add_fusion.place, bf16[512,1280]{1,0:T(8,128)(2,1)} %get-tuple-element.13.x_ref, bf16[4,3,160,512]{3,2,1,0:T(8,128)(2,1)S(1)} %pad_maximum_fusion.1.refs_0_, bf16[2,3,160,512]{3,2,1,0:T(8,128)(2,1)S(1)} %copy-done.3, bf16[1,3,160,512]{3,2,1,0:T(8,128)(2,1)S(1)} %bitcast.52, ...), custom_call_target="tpu_custom_call" | custom-call | flops 4026531840 | bytes 7864320 | tf_op jit(solution)/shard_map/pallas_call | solution.py:345
  236.2 7.5 %shard_map.137.refs_8_ = f32[512,1280]{1,0:T(8,128)S(1)} custom-call(s32[4]{0:T(128)S(1)} %pad_add_fusion.place, bf16[512,1280]{1,0:T(8,128)(2,1)} %collective-permute-done.37.x_ref, bf16[4,3,160,512]{3,2,1,0:T(8,128)(2,1)S(1)} %pad_maximum_fusion.1.refs_0_, bf16[2,3,160,512]{3,2,1,0:T(8,128)(2,1)S(1)} %copy-done.3, bf16[1,3,160,512]{3,2,1,0:T(8,128)(2,1)S(1)} %bitcast.53, ...), custom_call_target="tpu_custom_call" | custom-call | flops 4026531840 | bytes 7864320 | tf_op jit(solution)/shard_map/pallas_call | solution.py:345
  243.8 11.2 %shard_map.138 = bf16[512,1280]{1,0:T(8,128)(2,1)S(1)} custom-call(s32[4]{0:T(128)S(1)} %pad_add_fusion.place, bf16[512,1280]{1,0:T(8,128)(2,1)} %collective-permute-done.37.x_ref, bf16[4,3,160,768]{3,2,1,0:T(8,128)(2,1)} %pad_maximum_fusion.refs_0_, bf16[2,3,160,768]{3,2,1,0:T(8,128)(2,1)} %pad_maximum_fusion.2.refs_1_, ...), custom_call_target="tpu_custom_call" | custom-call | flops 6039797760 | bytes 11796480 | tf_op jit(solution)/shard_map/pallas_call | solution.py:345
  255.9 11.0 %shard_map.136 = f32[512,1280]{1,0:T(8,128)S(1)} custom-call(s32[4]{0:T(128)S(1)} %pad_add_fusion.place, bf16[512,1280]{1,0:T(8,128)(2,1)} %get-tuple-element.13.x_ref, bf16[4,3,160,768]{3,2,1,0:T(8,128)(2,1)} %pad_maximum_fusion.refs_0_, bf16[2,3,160,768]{3,2,1,0:T(8,128)(2,1)} %pad_maximum_fusion.2.refs_1_, bf16[1,3,160,768]{3,2,1,0:T(8,128)(2,1)S(1)} %bitcast.47, ...), custom_call_target="tpu_custom_call" | custom-call | flops 6039797760 | bytes 11796480 | tf_op jit(solution)/shard_map/pallas_call | solution.py:345
  268.2 17.5 %collective-permute-done.38 = bf16[512,1280]{1,0:T(8,128)(2,1)S(1)} collective-permute-done((bf16[512,1280]{1,0:T(8,128)(2,1)S(1)}, bf16[512,1280]{1,0:T(8,128)(2,1)S(1)}, u32[]{:S(2)}, u32[]{:S(2)}) %collective-permute-start.38) | collective-permute-done | bytes 1310752 | tf_op jit(solution)/shard_map/ppermute | solution.py:247
  285.7 2.7 fusion.8
  296.1 1.8 collective-permute-done.42
  298.1 2.8 collective-permute-start.44
  302.6 3.7 %collective-permute-done.45 = f32[8,128]{1,0:T(8,128)S(1)} collective-permute-done((f32[8,128]{1,0:T(8,128)S(1)}, f32[8,128]{1,0:T(8,128)S(1)}, u32[]{:S(2)}, u32[]{:S(2)}) %collective-permute-start.45) | collective-permute-done | bytes 4128 | tf_op jit(solution)/shard_map/ppermute | solution.py:244
  (163 shorter events, 60.2 us)
Async XLA Ops:
  5.4 60.9 %collective-permute-start.14 = (bf16[3,80,1280]{2,1,0:T(8,128)(2,1)}, bf16[3,80,1280]{2,1,0:T(8,128)(2,1)S(1)}, u32[]{:S(2)}, u32[]{:S(2)}) collective-permute-start(bf16[3,80,1280]{2,1,0:T(8,128)(2,1)} %constant_dynamic-slice_fusion), channel_id=1, source_target_pairs={{0,2},{2,0},{4,6},{6,4},{8,10},{10,8},{12,14},{14,12},{16,18},{18,... | collective-permute-start | bytes 1843208 | tf_op jit(solution)/shard_map/ppermute | solution.py:244
  10.9 25.8 %collective-permute-start.2 = (bf16[2,160,640]{2,1,0:T(8,128)(2,1)S(1)}, bf16[2,160,640]{2,1,0:T(8,128)(2,1)S(1)}, u32[]{:S(2)}, u32[]{:S(2)}) collective-permute-start(bf16[2,160,640]{2,1,0:T(8,128)(2,1)S(1)} %pad_maximum_fusion.6), channel_id=1, source_target_pairs={{0,8},{2,10},{4,12},{6,14},{8,0},{10,2},{12,4},{14,6},{16,24},{18,... | collective-permute-start | bytes 1228808 | tf_op jit(solution)/shard_map/ppermute | solution.py:244
  13.9 20.8 %collective-permute-start.3 = (bf16[2,160,640]{2,1,0:T(8,128)(2,1)S(1)}, bf16[2,160,640]{2,1,0:T(8,128)(2,1)S(1)}, u32[]{:S(2)}, u32[]{:S(2)}) collective-permute-start(bf16[2,160,640]{2,1,0:T(8,128)(2,1)S(1)} %pad_maximum_fusion.6), channel_id=1, source_target_pairs={{0,16},{2,18},{4,20},{6,22},{8,24},{10,26},{12,28},{14,30},{16,0},... | collective-permute-start | bytes 1228808 | tf_op jit(solution)/shard_map/ppermute | solution.py:244
  17.0 29.2 %collective-permute-start.5 = (bf16[2,160,640]{2,1,0:T(8,128)(2,1)S(1)}, bf16[2,160,640]{2,1,0:T(8,128)(2,1)S(1)}, u32[]{:S(2)}, u32[]{:S(2)}) collective-permute-start(bf16[2,160,640]{2,1,0:T(8,128)(2,1)S(1)} %pad_maximum_fusion.6), channel_id=1, source_target_pairs={{0,4},{2,6},{4,0},{6,2},{8,12},{10,14},{12,8},{14,10},{16,20},{18,... | collective-permute-start | bytes 1228808 | tf_op jit(solution)/shard_map/ppermute | solution.py:244
  35.2 21.9 %collective-permute-start.7 = (bf16[2,160,640]{2,1,0:T(8,128)(2,1)S(1)}, bf16[2,160,640]{2,1,0:T(8,128)(2,1)S(1)}, u32[]{:S(2)}, u32[]{:S(2)}) collective-permute-start(bf16[2,160,640]{2,1,0:T(8,128)(2,1)S(1)} %collective-permute-done.3), channel_id=1, source_target_pairs={{0,4},{2,6},{4,0},{6,2},{8,12},{10,14},{12,8},{14,10},{16,20},{18,... | collective-permute-start | bytes 1228808 | tf_op jit(solution)/shard_map/ppermute | solution.py:244
  36.7 19.6 %collective-permute-start.6 = (bf16[2,160,640]{2,1,0:T(8,128)(2,1)S(1)}, bf16[2,160,640]{2,1,0:T(8,128)(2,1)S(1)}, u32[]{:S(2)}, u32[]{:S(2)}) collective-permute-start(bf16[2,160,640]{2,1,0:T(8,128)(2,1)S(1)} %collective-permute-done.2), channel_id=1, source_target_pairs={{0,4},{2,6},{4,0},{6,2},{8,12},{10,14},{12,8},{14,10},{16,20},{18,... | collective-permute-start | bytes 1228808 | tf_op jit(solution)/shard_map/ppermute | solution.py:244
  43.9 19.0 %collective-permute-start.8 = (bf16[2,160,640]{2,1,0:T(8,128)(2,1)S(1)}, bf16[2,160,640]{2,1,0:T(8,128)(2,1)S(1)}, u32[]{:S(2)}, u32[]{:S(2)}) collective-permute-start(bf16[2,160,640]{2,1,0:T(8,128)(2,1)S(1)} %collective-permute-done.4), channel_id=1, source_target_pairs={{0,4},{2,6},{4,0},{6,2},{8,12},{10,14},{12,8},{14,10},{16,20},{18,... | collective-permute-start | bytes 1228808 | tf_op jit(solution)/shard_map/ppermute | solution.py:244
  63.7 43.9 %collective-permute-start.10 = (bf16[8,160,640]{2,1,0:T(8,128)(2,1)}, bf16[8,160,640]{2,1,0:T(8,128)(2,1)}, u32[]{:S(2)}, u32[]{:S(2)}) collective-permute-start(bf16[8,160,640]{2,1,0:T(8,128)(2,1)} %get-tuple-element.28.refs_1_.packed), channel_id=1, source_target_pairs={{0,2},{2,0},{4,6},{6,4},{8,10},{10,8},{12,14},{14,12},{16,18},{18,... | collective-permute-start | bytes 4915208 | tf_op jit(solution)/shard_map/ppermute | solution.py:244
  63.7 45.9 %collective-permute-start.9 = (bf16[8,160,640]{2,1,0:T(8,128)(2,1)}, bf16[8,160,640]{2,1,0:T(8,128)(2,1)}, u32[]{:S(2)}, u32[]{:S(2)}) collective-permute-start(bf16[8,160,640]{2,1,0:T(8,128)(2,1)} %get-tuple-element.29.refs_0_), channel_id=1, source_target_pairs={{0,2},{2,0},{4,6},{6,4},{8,10},{10,8},{12,14},{14,12},{16,18},{18,... | collective-permute-start | bytes 4915208 | tf_op jit(solution)/shard_map/ppermute | solution.py:244
  64.7 41.4 %collective-permute-start = (bf16[512,1280]{1,0:T(8,128)(2,1)S(1)}, bf16[512,1280]{1,0:T(8,128)(2,1)}, u32[]{:S(2)}, u32[]{:S(2)}) collective-permute-start(bf16[512,1280]{1,0:T(8,128)(2,1)S(1)} %fusion.4.n_own), channel_id=1, source_target_pairs={{0,1},{1,0},{2,3},{3,2},{4,5},{5,4},{6,7},{7,6},{8,9},{9,8},{10,11... | collective-permute-start | bytes 3932168 | tf_op jit(solution)/shard_map/ppermute | solution.py:247
  68.4 24.4 %collective-permute-start.27 = (bf16[3,160,512]{2,1,0:T(8,128)(2,1)}, bf16[3,160,512]{2,1,0:T(8,128)(2,1)}, u32[]{:S(2)}, u32[]{:S(2)}) collective-permute-start(bf16[3,160,512]{2,1,0:T(8,128)(2,1)} %get-tuple-element.27), channel_id=1, source_target_pairs={{0,16},{2,18},{4,20},{6,22},{8,24},{10,26},{12,28},{14,30},{16,0},... | collective-permute-start | bytes 1474568 | tf_op jit(solution)/shard_map/ppermute | solution.py:244
  70.8 24.8 %collective-permute-start.26 = (bf16[3,160,512]{2,1,0:T(8,128)(2,1)}, bf16[3,160,512]{2,1,0:T(8,128)(2,1)S(1)}, u32[]{:S(2)}, u32[]{:S(2)}) collective-permute-start(bf16[3,160,512]{2,1,0:T(8,128)(2,1)} %get-tuple-element.27), channel_id=1, source_target_pairs={{0,8},{2,10},{4,12},{6,14},{8,0},{10,2},{12,4},{14,6},{16,24},{18,... | collective-permute-start | bytes 1474568 | tf_op jit(solution)/shard_map/ppermute | solution.py:244
  95.6 33.6 %collective-permute-start.16 = (bf16[3,160,768]{2,1,0:T(8,128)(2,1)S(1)}, bf16[3,160,768]{2,1,0:T(8,128)(2,1)S(1)}, u32[]{:S(2)}, u32[]{:S(2)}) collective-permute-start(bf16[3,160,768]{2,1,0:T(8,128)(2,1)S(1)} %get-tuple-element.23), channel_id=1, source_target_pairs={{0,16},{2,18},{4,20},{6,22},{8,24},{10,26},{12,28},{14,30},{16,0},... | collective-permute-start | bytes 2211848 | tf_op jit(solution)/shard_map/ppermute | solution.py:244
  106.1 35.1 %collective-permute-start.15 = (bf16[3,160,768]{2,1,0:T(8,128)(2,1)S(1)}, bf16[3,160,768]{2,1,0:T(8,128)(2,1)S(1)}, u32[]{:S(2)}, u32[]{:S(2)}) collective-permute-start(bf16[3,160,768]{2,1,0:T(8,128)(2,1)S(1)} %get-tuple-element.23), channel_id=1, source_target_pairs={{0,8},{2,10},{4,12},{6,14},{8,0},{10,2},{12,4},{14,6},{16,24},{18,... | collective-permute-start | bytes 2211848 | tf_op jit(solution)/shard_map/ppermute | solution.py:244
  106.1 36.5 %collective-permute-start.18 = (bf16[3,160,768]{2,1,0:T(8,128)(2,1)S(1)}, bf16[3,160,768]{2,1,0:T(8,128)(2,1)S(1)}, u32[]{:S(2)}, u32[]{:S(2)}) collective-permute-start(bf16[3,160,768]{2,1,0:T(8,128)(2,1)S(1)} %get-tuple-element.23), channel_id=1, source_target_pairs={{0,4},{2,6},{4,0},{6,2},{8,12},{10,14},{12,8},{14,10},{16,20},{18,... | collective-permute-start | bytes 2211848 | tf_op jit(solution)/shard_map/ppermute | solution.py:244
  107.6 44.1 %collective-permute-start.28 = (bf16[3,160,512]{2,1,0:T(8,128)(2,1)}, bf16[3,160,512]{2,1,0:T(8,128)(2,1)S(1)}, u32[]{:S(2)}, u32[]{:S(2)}) collective-permute-start(bf16[3,160,512]{2,1,0:T(8,128)(2,1)} %collective-permute-done.27), channel_id=1, source_target_pairs={{0,8},{2,10},{4,12},{6,14},{8,0},{10,2},{12,4},{14,6},{16,24},{18,... | collective-permute-start | bytes 1474568 | tf_op jit(solution)/shard_map/ppermute | solution.py:244
  109.6 56.0 %collective-permute-start.12 = (bf16[8,160,640]{2,1,0:T(8,128)(2,1)}, bf16[8,160,640]{2,1,0:T(8,128)(2,1)S(1)}, u32[]{:S(2)}, u32[]{:S(2)}) collective-permute-start(bf16[8,160,640]{2,1,0:T(8,128)(2,1)} %get-tuple-element.28.refs_1_.packed), channel_id=1, source_target_pairs={{2,3},{3,2},{6,7},{7,6},{10,11},{11,10},{14,15},{15,14},{18,19},{1... | collective-permute-start | bytes 4915208 | tf_op jit(solution)/shard_map/ppermute | solution.py:323
  129.2 34.1 %collective-permute-start.30 = (bf16[3,160,512]{2,1,0:T(8,128)(2,1)}, bf16[3,160,512]{2,1,0:T(8,128)(2,1)S(1)}, u32[]{:S(2)}, u32[]{:S(2)}) collective-permute-start(bf16[3,160,512]{2,1,0:T(8,128)(2,1)} %collective-permute-done.27), channel_id=1, source_target_pairs={{0,4},{2,6},{4,0},{6,2},{8,12},{10,14},{12,8},{14,10},{16,20},{18,... | collective-permute-start | bytes 1474568 | tf_op jit(solution)/shard_map/ppermute | solution.py:244
  141.2 22.7 %collective-permute-start.31 = (bf16[3,160,512]{2,1,0:T(8,128)(2,1)S(1)}, bf16[3,160,512]{2,1,0:T(8,128)(2,1)S(1)}, u32[]{:S(2)}, u32[]{:S(2)}) collective-permute-start(bf16[3,160,512]{2,1,0:T(8,128)(2,1)S(1)} %collective-permute-done.26), channel_id=1, source_target_pairs={{0,4},{2,6},{4,0},{6,2},{8,12},{10,14},{12,8},{14,10},{16,20},{18,... | collective-permute-start | bytes 1474568 | tf_op jit(solution)/shard_map/ppermute | solution.py:244
  142.7 23.0 %collective-permute-start.17 = (bf16[3,160,768]{2,1,0:T(8,128)(2,1)S(1)}, bf16[3,160,768]{2,1,0:T(8,128)(2,1)S(1)}, u32[]{:S(2)}, u32[]{:S(2)}) collective-permute-start(bf16[3,160,768]{2,1,0:T(8,128)(2,1)S(1)} %collective-permute-done.16), channel_id=1, source_target_pairs={{0,8},{2,10},{4,12},{6,14},{8,0},{10,2},{12,4},{14,6},{16,24},{18,... | collective-permute-start | bytes 2211848 | tf_op jit(solution)/shard_map/ppermute | solution.py:244
  151.7 29.0 %collective-permute-start.19 = (bf16[3,160,768]{2,1,0:T(8,128)(2,1)S(1)}, bf16[3,160,768]{2,1,0:T(8,128)(2,1)}, u32[]{:S(2)}, u32[]{:S(2)}) collective-permute-start(bf16[3,160,768]{2,1,0:T(8,128)(2,1)S(1)} %collective-permute-done.16), channel_id=1, source_target_pairs={{0,4},{2,6},{4,0},{6,2},{8,12},{10,14},{12,8},{14,10},{16,20},{18,... | collective-permute-start | bytes 2211848 | tf_op jit(solution)/shard_map/ppermute | solution.py:244
  165.6 25.8 %collective-permute-start.13 = (bf16[8,160,640]{2,1,0:T(8,128)(2,1)S(1)}, bf16[8,160,640]{2,1,0:T(8,128)(2,1)S(1)}, u32[]{:S(2)}, u32[]{:S(2)}) collective-permute-start(bf16[8,160,640]{2,1,0:T(8,128)(2,1)S(1)} %collective-permute-done.12.y_own), channel_id=1, source_target_pairs={{2,0},{6,4},{10,8},{14,12},{18,16},{22,20},{26,24},{30,28},{3,1},{... | collective-permute-start | bytes 4915208 | tf_op jit(solution)/shard_map/ppermute | solution.py:326
  179.4 21.5 %collective-permute-start.20 = (bf16[3,160,768]{2,1,0:T(8,128)(2,1)S(1)}, bf16[3,160,768]{2,1,0:T(8,128)(2,1)S(1)}, u32[]{:S(2)}, u32[]{:S(2)}) collective-permute-start(bf16[3,160,768]{2,1,0:T(8,128)(2,1)S(1)} %collective-permute-done.15), channel_id=1, source_target_pairs={{0,4},{2,6},{4,0},{6,2},{8,12},{10,14},{12,8},{14,10},{16,20},{18,... | collective-permute-start | bytes 2211848 | tf_op jit(solution)/shard_map/ppermute | solution.py:244
  180.7 40.8 %collective-permute-start.33 = (bf16[4,3,160,512]{3,2,1,0:T(8,128)(2,1)S(1)}, bf16[4,3,160,512]{3,2,1,0:T(8,128)(2,1)}, u32[]{:S(2)}, u32[]{:S(2)}) collective-permute-start(bf16[4,3,160,512]{3,2,1,0:T(8,128)(2,1)S(1)} %pad_maximum_fusion.1.refs_0_), channel_id=1, source_target_pairs={{0,2},{2,0},{4,6},{6,4},{8,10},{10,8},{12,14},{14,12},{16,18},{18,... | collective-permute-start | bytes 5898248 | tf_op jit(solution)/shard_map/ppermute | solution.py:244
  180.7 20.6 %collective-permute-start.34 = (bf16[2,3,160,512]{3,2,1,0:T(8,128)(2,1)S(1)}, bf16[2,3,160,512]{3,2,1,0:T(8,128)(2,1)S(1)}, u32[]{:S(2)}, u32[]{:S(2)}) collective-permute-start(bf16[2,3,160,512]{3,2,1,0:T(8,128)(2,1)S(1)} %pad_maximum_fusion.4.refs_1_), channel_id=1, source_target_pairs={{0,2},{2,0},{4,6},{6,4},{8,10},{10,8},{12,14},{14,12},{16,18},{18,... | collective-permute-start | bytes 2949128 | tf_op jit(solution)/shard_map/ppermute | solution.py:244
  181.3 62.5 %collective-permute-start.22 = (bf16[4,3,160,768]{3,2,1,0:T(8,128)(2,1)}, bf16[4,3,160,768]{3,2,1,0:T(8,128)(2,1)}, u32[]{:S(2)}, u32[]{:S(2)}) collective-permute-start(bf16[4,3,160,768]{3,2,1,0:T(8,128)(2,1)} %pad_maximum_fusion.refs_0_), channel_id=1, source_target_pairs={{0,2},{2,0},{4,6},{6,4},{8,10},{10,8},{12,14},{14,12},{16,18},{18,... | collective-permute-start | bytes 8847368 | tf_op jit(solution)/shard_map/ppermute | solution.py:244
  200.9 35.3 %collective-permute-start.37 = (bf16[512,1280]{1,0:T(8,128)(2,1)}, bf16[512,1280]{1,0:T(8,128)(2,1)}, u32[]{:S(2)}, u32[]{:S(2)}) collective-permute-start(bf16[512,1280]{1,0:T(8,128)(2,1)} %get-tuple-element.13.x_ref), channel_id=1, source_target_pairs={{0,1},{1,0},{2,3},{3,2},{4,5},{5,4},{6,7},{7,6},{8,9},{9,8},{10,11... | collective-permute-start | bytes 3932168 | tf_op jit(solution)/shard_map/ppermute | solution.py:247
  202.7 18.8 %collective-permute-start.21 = (bf16[3,160,768]{2,1,0:T(8,128)(2,1)}, bf16[3,160,768]{2,1,0:T(8,128)(2,1)}, u32[]{:S(2)}, u32[]{:S(2)}) collective-permute-start(bf16[3,160,768]{2,1,0:T(8,128)(2,1)} %collective-permute-done.19), channel_id=1, source_target_pairs={{0,8},{2,10},{4,12},{6,14},{8,0},{10,2},{12,4},{14,6},{16,24},{18,... | collective-permute-start | bytes 2211848 | tf_op jit(solution)/shard_map/ppermute | solution.py:244
  205.9 37.8 %collective-permute-start.23 = (bf16[2,3,160,768]{3,2,1,0:T(8,128)(2,1)}, bf16[2,3,160,768]{3,2,1,0:T(8,128)(2,1)}, u32[]{:S(2)}, u32[]{:S(2)}) collective-permute-start(bf16[2,3,160,768]{3,2,1,0:T(8,128)(2,1)} %pad_maximum_fusion.2.refs_1_), channel_id=1, source_target_pairs={{0,2},{2,0},{4,6},{6,4},{8,10},{10,8},{12,14},{14,12},{16,18},{18,... | collective-permute-start | bytes 4423688 | tf_op jit(solution)/shard_map/ppermute | solution.py:244
  221.5 22.2 %collective-permute-start.24 = (bf16[3,160,768]{2,1,0:T(8,128)(2,1)}, bf16[3,160,768]{2,1,0:T(8,128)(2,1)S(1)}, u32[]{:S(2)}, u32[]{:S(2)}) collective-permute-start(bf16[3,160,768]{2,1,0:T(8,128)(2,1)} %copy-done.7), channel_id=1, source_target_pairs={{0,2},{2,0},{4,6},{6,4},{8,10},{10,8},{12,14},{14,12},{16,18},{18,... | collective-permute-start | bytes 2211848 | tf_op jit(solution)/shard_map/ppermute | solution.py:244
  221.5 22.2 %collective-permute-start.25 = (bf16[3,160,768]{2,1,0:T(8,128)(2,1)}, bf16[3,160,768]{2,1,0:T(8,128)(2,1)S(1)}, u32[]{:S(2)}, u32[]{:S(2)}) collective-permute-start(bf16[3,160,768]{2,1,0:T(8,128)(2,1)} %collective-permute-done.21), channel_id=1, source_target_pairs={{0,2},{2,0},{4,6},{6,4},{8,10},{10,8},{12,14},{14,12},{16,18},{18,... | collective-permute-start | bytes 2211848 | tf_op jit(solution)/shard_map/ppermute | solution.py:244
  255.0 30.7 %collective-permute-start.38 = (bf16[512,1280]{1,0:T(8,128)(2,1)S(1)}, bf16[512,1280]{1,0:T(8,128)(2,1)S(1)}, u32[]{:S(2)}, u32[]{:S(2)}) collective-permute-start(bf16[512,1280]{1,0:T(8,128)(2,1)S(1)} %shard_map.138), channel_id=1, source_target_pairs={{0,1},{1,0},{2,3},{3,2},{4,5},{5,4},{6,7},{7,6},{8,9},{9,8},{10,11... | collective-permute-start | bytes 3932168 | tf_op jit(solution)/shard_map/ppermute | solution.py:247
  (43 other events, 277.7 us)

commit v2 on v1

--- a/solution.py
+++ b/solution.py
@@ -104,25 +104,30 @@
 def qkv_body(scale, lines, place, n_own, n_peer, *refs):
     q_own, q_peer, k_out, v_out, w, sems = refs[4:]
     rows = refs[0].shape[1]
-    copies = []
-    for number, ref in enumerate(refs[:4]):
-        slot = (place[2] ^ (number // 2)) * 2 + number % 2
-        for index in range(ref.shape[0]):
+    pieces = refs[0].shape[0]
+
+    def each(number, slot, act):
+        for index in range(pieces):
             base = pl.ds(piece_base(place, index, lines, rows), rows)
-            copies.append(pltpu.make_async_copy(ref.at[index], w.at[slot, base, :], sems.at[number // 2]))
-    for cp in copies:
-        cp.start()
-    for cp in copies:
-        cp.wait()
+            act(pltpu.make_async_copy(refs[number].at[index], w.at[slot, base, :], sems.at[slot]))
+
+    for mat in range(2):
+        for number in (mat, mat + 2):
+            slot = (place[2] ^ (number // 2)) * 2 + mat
+
+            @pl.when(slot < 3)
+            def _(number=number, slot=slot):
+                each(number, slot, lambda cp: cp.start())
+
     half = n_own.shape[0]
     block = 256
     pairs = k_out.shape[0]
-    for which, src in enumerate((n_own, n_peer)):
-        for t in range(half // block):
-            a = src[t * block : (t + 1) * block, :]
-            lo = t * block
-            for mat in range(3):
-                r = dot(a, w[mat]).astype(BF16)
+    for mat in range(3):
+        each(0, mat, lambda cp: cp.wait())
+        for which, src in enumerate((n_own, n_peer)):
+            for t in range(half // block):
+                lo = t * block
+                r = dot(src[lo : lo + block, :], w[mat]).astype(BF16)
                 if mat == 0:
                     r = r * jnp.asarray(scale, BF16)
                 for p in range(pairs):
@@ -304,8 +309,8 @@
         [half_shape, half_shape, full_shape, full_shape],
         [smem_spec(), vmem_spec(), vmem_spec()] + [hbm_spec()] * 4,
         [
-            pltpu.VMEM((4, width, heads_width), BF16),
-            pltpu.SemaphoreType.DMA((2,)),
+            pltpu.VMEM((3, width, heads_width), BF16),
+            pltpu.SemaphoreType.DMA((3,)),
         ],
         8 * 10**9,
         wbytes + 8 * rows * width,

time: 308 us -> 308 us (level)
  no operation moved by 1% of the time
where the time goes in v2:
time: 308 us; the launch traced here: 307 us
  waiting for transfers between devices  147 us (48%)
  Pallas kernels  74.9 us (24%)
  starting transfers between devices  39.9 us (13%)
  other arithmetic  22.3 us (7%)
  local copies, waits for them, and re-layouts  17.6 us (6%)
  between operations  5.04 us (2%)
    ppermute x38, waiting for transfers between devices, flip(): return lax.ppermute(value, 'dp', [(i, i ^ bits) for i in range(dp)])  126 us
    pallas_call x4, Pallas kernels, ff(): call(functools.partial(ff_body, acc is not None, groups, lines), [jax.Sha...  37.3 us
    ppermute x38, starting transfers between devices, flip(): return lax.ppermute(value, 'dp', [(i, i ^ bits) for i in range(dp)])  32.3 us
    pallas_call x2, Pallas kernels, attend(): call(attn_body, [half_shape], [vmem_spec()] * 3, [], 12 * 10 ** 9, 8 * ro...  20.2 us
    ppermute x5, waiting for transfers between devices, flip_y(): return lax.ppermute(value, 'mp', [(0, 1), (1, 0)])  19 us
    unnamed x64, local copies, waits for them, and re-layouts  15.3 us
    pallas_call x1, Pallas kernels, fast_shards(): call(functools.partial(qkv_body, scale, lines), [half_shape, half_shape,...  9.55 us
    pallas_call x1, Pallas kernels, fast_shards(): call(functools.partial(wout_body, lines), [jax.ShapeDtypeStruct((rows, wi...  7.8 us
  transfers between devices with their start and end apart: 46, of which 19 were waited for; matrix products, arithmetic and copies ran while one was open for 8% of the time, Pallas kernels for 21%

profile of v2, /device:TPU:0, one launch (start us, length us, event | category | flops | bytes accessed | tf_op | source)
XLA Modules:
  0.0 306.8 jit_solution(14061037381726615912)
XLA Ops:
  0.6 1.7 fusion.11
  8.0 2.6 convert_reduce_fusion
  10.9 3.1 %collective-permute-start.2 = (bf16[2,160,640]{2,1,0:T(8,128)(2,1)S(1)}, bf16[2,160,640]{2,1,0:T(8,128)(2,1)S(1)}, u32[]{:S(2)}, u32[]{:S(2)}) collective-permute-start(bf16[2,160,640]{2,1,0:T(8,128)(2,1)S(1)} %pad_maximum_fusion.6), channel_id=1, source_target_pairs={{0,8},{2,10},{4,12},{6,14},{8,0},{10,2},{12,4},{14,6},{16,24},{18,... | collective-permute-start | bytes 1228808 | tf_op jit(solution)/shard_map/ppermute | solution.py:249
  13.9 2.6 collective-permute-start.3
  19.4 15.4 %collective-permute-done.3 = bf16[2,160,640]{2,1,0:T(8,128)(2,1)S(1)} collective-permute-done((bf16[2,160,640]{2,1,0:T(8,128)(2,1)S(1)}, bf16[2,160,640]{2,1,0:T(8,128)(2,1)S(1)}, u32[]{:S(2)}, u32[]{:S(2)}) %collective-permute-start.3) | collective-permute-done | bytes 409632 | tf_op jit(solution)/shard_map/ppermute | solution.py:249
  38.8 5.1 %collective-permute-done.4 = bf16[2,160,640]{2,1,0:T(8,128)(2,1)S(1)} collective-permute-done((bf16[2,160,640]{2,1,0:T(8,128)(2,1)S(1)}, bf16[2,160,640]{2,1,0:T(8,128)(2,1)S(1)}, u32[]{:S(2)}, u32[]{:S(2)}) %collective-permute-start.4) | collective-permute-done | bytes 409632 | tf_op jit(solution)/shard_map/ppermute | solution.py:249
  47.0 9.3 %collective-permute-done.6 = bf16[2,160,640]{2,1,0:T(8,128)(2,1)S(1)} collective-permute-done((bf16[2,160,640]{2,1,0:T(8,128)(2,1)S(1)}, bf16[2,160,640]{2,1,0:T(8,128)(2,1)S(1)}, u32[]{:S(2)}, u32[]{:S(2)}) %collective-permute-start.6) | collective-permute-done | bytes 409632 | tf_op jit(solution)/shard_map/ppermute | solution.py:249
  57.9 5.1 %collective-permute-done.8 = bf16[2,160,640]{2,1,0:T(8,128)(2,1)S(1)} collective-permute-done((bf16[2,160,640]{2,1,0:T(8,128)(2,1)S(1)}, bf16[2,160,640]{2,1,0:T(8,128)(2,1)S(1)}, u32[]{:S(2)}, u32[]{:S(2)}) %collective-permute-start.8) | collective-permute-done | bytes 409632 | tf_op jit(solution)/shard_map/ppermute | solution.py:249
  68.4 2.4 collective-permute-start.27
  71.1 21.7 %collective-permute-done.27 = bf16[3,160,512]{2,1,0:T(8,128)(2,1)} collective-permute-done((bf16[3,160,512]{2,1,0:T(8,128)(2,1)}, bf16[3,160,512]{2,1,0:T(8,128)(2,1)}, u32[]{:S(2)}, u32[]{:S(2)}) %collective-permute-start.27) | collective-permute-done | bytes 491552 | tf_op jit(solution)/shard_map/ppermute | solution.py:249
  95.7 10.4 %collective-permute-done.29 = bf16[3,160,512]{2,1,0:T(8,128)(2,1)S(1)} collective-permute-done((bf16[3,160,512]{2,1,0:T(8,128)(2,1)}, bf16[3,160,512]{2,1,0:T(8,128)(2,1)S(1)}, u32[]{:S(2)}, u32[]{:S(2)}) %collective-permute-start.29) | collective-permute-done | bytes 491552 | tf_op jit(solution)/shard_map/ppermute | solution.py:249
  107.6 2.0 collective-permute-start.28
  110.4 9.5 %shard_map.131 = (bf16[5,512,128]{2,1,0:T(8,128)(2,1)S(1)}, bf16[5,512,128]{2,1,0:T(8,128)(2,1)S(1)}, bf16[5,1024,128]{2,1,0:T(8,128)(2,1)S(1)}, bf16[5,1024,128]{2,1,0:T(8,128)(2,1)S(1)}) custom-call(s32[4]{0:T(128)S(1)} %pad_add_fusion.place, bf16[512,1280]{1,0:T(8,128)(2,1)S(1)} %fusion.4.n_own, bf16[512,1280]{1,0:T(8,128)(2,1)} %collective-permute-done.n_peer, ...), custom_call_target="tpu_custom_call" | custom-call | flops 8000000000 | bytes 11796480 | tf_op jit(solution)/shard_map/pallas_call | solution.py:307
  120.0 9.3 %collective-permute-done.16 = bf16[3,160,768]{2,1,0:T(8,128)(2,1)S(1)} collective-permute-done((bf16[3,160,768]{2,1,0:T(8,128)(2,1)S(1)}, bf16[3,160,768]{2,1,0:T(8,128)(2,1)S(1)}, u32[]{:S(2)}, u32[]{:S(2)}) %collective-permute-start.16) | collective-permute-done | bytes 737312 | tf_op jit(solution)/shard_map/ppermute | solution.py:249
  129.8 11.4 %collective-permute-done.15 = bf16[3,160,768]{2,1,0:T(8,128)(2,1)S(1)} collective-permute-done((bf16[3,160,768]{2,1,0:T(8,128)(2,1)S(1)}, bf16[3,160,768]{2,1,0:T(8,128)(2,1)S(1)}, u32[]{:S(2)}, u32[]{:S(2)}) %collective-permute-start.15) | collective-permute-done | bytes 737312 | tf_op jit(solution)/shard_map/ppermute | solution.py:249
  142.7 9.0 %collective-permute-done.28 = bf16[3,160,512]{2,1,0:T(8,128)(2,1)S(1)} collective-permute-done((bf16[3,160,512]{2,1,0:T(8,128)(2,1)}, bf16[3,160,512]{2,1,0:T(8,128)(2,1)S(1)}, u32[]{:S(2)}, u32[]{:S(2)}) %collective-permute-start.28) | collective-permute-done | bytes 491552 | tf_op jit(solution)/shard_map/ppermute | solution.py:249
  153.2 10.1 %shard_map.133 = bf16[5,512,128]{2,1,0:T(8,128)(2,1)S(1)} custom-call(bf16[5,512,128]{2,1,0:T(8,128)(2,1)S(1)} %get-tuple-element.11.q_ref, bf16[5,1024,128]{2,1,0:T(8,128)(2,1)S(1)} %get-tuple-element.9.k_ref, bf16[5,1024,128]{2,1,0:T(8,128)(2,1)S(1)} %get-tuple-element.10.v_ref), custom_call_target="tpu_custom_call" | custom-call | flops 12000000000 | bytes 5242880 | tf_op jit(solution)/shard_map/pallas_call | solution.py:320
  168.7 1.8 pad_maximum_fusion.refs_0_
  170.5 8.9 %collective-permute-done.32 = bf16[3,160,512]{2,1,0:T(8,128)(2,1)S(1)} collective-permute-done((bf16[3,160,512]{2,1,0:T(8,128)(2,1)S(1)}, bf16[3,160,512]{2,1,0:T(8,128)(2,1)S(1)}, u32[]{:S(2)}, u32[]{:S(2)}) %collective-permute-start.32) | collective-permute-done | bytes 491552 | tf_op jit(solution)/shard_map/ppermute | solution.py:249
  181.3 10.1 %shard_map.132.m_own = bf16[5,512,128]{2,1,0:T(8,128)(2,1)S(1)} custom-call(bf16[5,512,128]{2,1,0:T(8,128)(2,1)S(1)} %get-tuple-element.8.q_ref, bf16[5,1024,128]{2,1,0:T(8,128)(2,1)S(1)} %get-tuple-element.9.k_ref, bf16[5,1024,128]{2,1,0:T(8,128)(2,1)S(1)} %get-tuple-element.10.v_ref), custom_call_target="tpu_custom_call" | custom-call | flops 12000000000 | bytes 5242880 | tf_op jit(solution)/shard_map/pallas_call | solution.py:320
  192.0 7.8 %shard_map.134 = (bf16[512,1280]{1,0:T(8,128)(2,1)S(1)}, bf16[512,1280]{1,0:T(8,128)(2,1)}) custom-call(s32[4]{0:T(128)S(1)} %pad_add_fusion.place, f32[1,1280]{1,0:T(1,128)S(1)} %reshape.41.gain, bf16[512,1280]{1,0:T(8,128)(2,1)S(1)} %get-tuple-element.15.noised, bf16[5,512,128]{2,1,0:T(8,128)(2,1)S(1)} %shard_map.132.m_own, ...), custom_call_target="tpu_custom_call" | custom-call | flops 4000000000 | bytes 6553600 | tf_op jit(solution)/shard_map/pallas_call | solution.py:332
  202.7 2.4 pad_maximum_fusion.2.refs_1_
  207.3 14.2 %collective-permute-done.21 = bf16[3,160,768]{2,1,0:T(8,128)(2,1)} collective-permute-done((bf16[3,160,768]{2,1,0:T(8,128)(2,1)}, bf16[3,160,768]{2,1,0:T(8,128)(2,1)}, u32[]{:S(2)}, u32[]{:S(2)}) %collective-permute-start.21) | collective-permute-done | bytes 737312 | tf_op jit(solution)/shard_map/ppermute | solution.py:249
  228.6 7.6 %shard_map.135.refs_8_ = f32[512,1280]{1,0:T(8,128)S(1)} custom-call(s32[4]{0:T(128)S(1)} %pad_add_fusion.place, bf16[512,1280]{1,0:T(8,128)(2,1)} %get-tuple-element.13.x_ref, bf16[4,3,160,512]{3,2,1,0:T(8,128)(2,1)S(1)} %pad_maximum_fusion.1.refs_0_, bf16[2,3,160,512]{3,2,1,0:T(8,128)(2,1)S(1)} %copy-done.3, bf16[1,3,160,512]{3,2,1,0:T(8,128)(2,1)S(1)} %bitcast.52, ...), custom_call_target="tpu_custom_call" | custom-call | flops 4026531840 | bytes 7864320 | tf_op jit(solution)/shard_map/pallas_call | solution.py:350
  236.2 7.5 %shard_map.137.refs_8_ = f32[512,1280]{1,0:T(8,128)S(1)} custom-call(s32[4]{0:T(128)S(1)} %pad_add_fusion.place, bf16[512,1280]{1,0:T(8,128)(2,1)} %collective-permute-done.37.x_ref, bf16[4,3,160,512]{3,2,1,0:T(8,128)(2,1)S(1)} %pad_maximum_fusion.1.refs_0_, bf16[2,3,160,512]{3,2,1,0:T(8,128)(2,1)S(1)} %copy-done.3, bf16[1,3,160,512]{3,2,1,0:T(8,128)(2,1)S(1)} %bitcast.53, ...), custom_call_target="tpu_custom_call" | custom-call | flops 4026531840 | bytes 7864320 | tf_op jit(solution)/shard_map/pallas_call | solution.py:350
  243.8 11.2 %shard_map.138 = bf16[512,1280]{1,0:T(8,128)(2,1)S(1)} custom-call(s32[4]{0:T(128)S(1)} %pad_add_fusion.place, bf16[512,1280]{1,0:T(8,128)(2,1)} %collective-permute-done.37.x_ref, bf16[4,3,160,768]{3,2,1,0:T(8,128)(2,1)} %pad_maximum_fusion.refs_0_, bf16[2,3,160,768]{3,2,1,0:T(8,128)(2,1)} %pad_maximum_fusion.2.refs_1_, ...), custom_call_target="tpu_custom_call" | custom-call | flops 6039797760 | bytes 11796480 | tf_op jit(solution)/shard_map/pallas_call | solution.py:350
  255.9 11.0 %shard_map.136 = f32[512,1280]{1,0:T(8,128)S(1)} custom-call(s32[4]{0:T(128)S(1)} %pad_add_fusion.place, bf16[512,1280]{1,0:T(8,128)(2,1)} %get-tuple-element.13.x_ref, bf16[4,3,160,768]{3,2,1,0:T(8,128)(2,1)} %pad_maximum_fusion.refs_0_, bf16[2,3,160,768]{3,2,1,0:T(8,128)(2,1)} %pad_maximum_fusion.2.refs_1_, bf16[1,3,160,768]{3,2,1,0:T(8,128)(2,1)S(1)} %bitcast.47, ...), custom_call_target="tpu_custom_call" | custom-call | flops 6039797760 | bytes 11796480 | tf_op jit(solution)/shard_map/pallas_call | solution.py:350
  268.2 17.5 %collective-permute-done.38 = bf16[512,1280]{1,0:T(8,128)(2,1)S(1)} collective-permute-done((bf16[512,1280]{1,0:T(8,128)(2,1)S(1)}, bf16[512,1280]{1,0:T(8,128)(2,1)S(1)}, u32[]{:S(2)}, u32[]{:S(2)}) %collective-permute-start.38) | collective-permute-done | bytes 1310752 | tf_op jit(solution)/shard_map/ppermute | solution.py:252
  285.7 2.7 fusion.8
  296.1 1.8 collective-permute-done.42
  298.1 2.8 collective-permute-start.44
  302.6 3.7 %collective-permute-done.45 = f32[8,128]{1,0:T(8,128)S(1)} collective-permute-done((f32[8,128]{1,0:T(8,128)S(1)}, f32[8,128]{1,0:T(8,128)S(1)}, u32[]{:S(2)}, u32[]{:S(2)}) %collective-permute-start.45) | collective-permute-done | bytes 4128 | tf_op jit(solution)/shard_map/ppermute | solution.py:249
  (163 shorter events, 60.0 us)
Async XLA Ops:
  5.4 60.9 %collective-permute-start.14 = (bf16[3,80,1280]{2,1,0:T(8,128)(2,1)}, bf16[3,80,1280]{2,1,0:T(8,128)(2,1)S(1)}, u32[]{:S(2)}, u32[]{:S(2)}) collective-permute-start(bf16[3,80,1280]{2,1,0:T(8,128)(2,1)} %constant_dynamic-slice_fusion), channel_id=1, source_target_pairs={{0,2},{2,0},{4,6},{6,4},{8,10},{10,8},{12,14},{14,12},{16,18},{18,... | collective-permute-start | bytes 1843208 | tf_op jit(solution)/shard_map/ppermute | solution.py:249
  10.9 25.8 %collective-permute-start.2 = (bf16[2,160,640]{2,1,0:T(8,128)(2,1)S(1)}, bf16[2,160,640]{2,1,0:T(8,128)(2,1)S(1)}, u32[]{:S(2)}, u32[]{:S(2)}) collective-permute-start(bf16[2,160,640]{2,1,0:T(8,128)(2,1)S(1)} %pad_maximum_fusion.6), channel_id=1, source_target_pairs={{0,8},{2,10},{4,12},{6,14},{8,0},{10,2},{12,4},{14,6},{16,24},{18,... | collective-permute-start | bytes 1228808 | tf_op jit(solution)/shard_map/ppermute | solution.py:249
  13.9 20.8 %collective-permute-start.3 = (bf16[2,160,640]{2,1,0:T(8,128)(2,1)S(1)}, bf16[2,160,640]{2,1,0:T(8,128)(2,1)S(1)}, u32[]{:S(2)}, u32[]{:S(2)}) collective-permute-start(bf16[2,160,640]{2,1,0:T(8,128)(2,1)S(1)} %pad_maximum_fusion.6), channel_id=1, source_target_pairs={{0,16},{2,18},{4,20},{6,22},{8,24},{10,26},{12,28},{14,30},{16,0},... | collective-permute-start | bytes 1228808 | tf_op jit(solution)/shard_map/ppermute | solution.py:249
  17.0 29.2 %collective-permute-start.5 = (bf16[2,160,640]{2,1,0:T(8,128)(2,1)S(1)}, bf16[2,160,640]{2,1,0:T(8,128)(2,1)S(1)}, u32[]{:S(2)}, u32[]{:S(2)}) collective-permute-start(bf16[2,160,640]{2,1,0:T(8,128)(2,1)S(1)} %pad_maximum_fusion.6), channel_id=1, source_target_pairs={{0,4},{2,6},{4,0},{6,2},{8,12},{10,14},{12,8},{14,10},{16,20},{18,... | collective-permute-start | bytes 1228808 | tf_op jit(solution)/shard_map/ppermute | solution.py:249
  35.2 21.9 %collective-permute-start.7 = (bf16[2,160,640]{2,1,0:T(8,128)(2,1)S(1)}, bf16[2,160,640]{2,1,0:T(8,128)(2,1)S(1)}, u32[]{:S(2)}, u32[]{:S(2)}) collective-permute-start(bf16[2,160,640]{2,1,0:T(8,128)(2,1)S(1)} %collective-permute-done.3), channel_id=1, source_target_pairs={{0,4},{2,6},{4,0},{6,2},{8,12},{10,14},{12,8},{14,10},{16,20},{18,... | collective-permute-start | bytes 1228808 | tf_op jit(solution)/shard_map/ppermute | solution.py:249
  36.7 19.6 %collective-permute-start.6 = (bf16[2,160,640]{2,1,0:T(8,128)(2,1)S(1)}, bf16[2,160,640]{2,1,0:T(8,128)(2,1)S(1)}, u32[]{:S(2)}, u32[]{:S(2)}) collective-permute-start(bf16[2,160,640]{2,1,0:T(8,128)(2,1)S(1)} %collective-permute-done.2), channel_id=1, source_target_pairs={{0,4},{2,6},{4,0},{6,2},{8,12},{10,14},{12,8},{14,10},{16,20},{18,... | collective-permute-start | bytes 1228808 | tf_op jit(solution)/shard_map/ppermute | solution.py:249
  43.9 19.0 %collective-permute-start.8 = (bf16[2,160,640]{2,1,0:T(8,128)(2,1)S(1)}, bf16[2,160,640]{2,1,0:T(8,128)(2,1)S(1)}, u32[]{:S(2)}, u32[]{:S(2)}) collective-permute-start(bf16[2,160,640]{2,1,0:T(8,128)(2,1)S(1)} %collective-permute-done.4), channel_id=1, source_target_pairs={{0,4},{2,6},{4,0},{6,2},{8,12},{10,14},{12,8},{14,10},{16,20},{18,... | collective-permute-start | bytes 1228808 | tf_op jit(solution)/shard_map/ppermute | solution.py:249
  63.7 43.9 %collective-permute-start.10 = (bf16[8,160,640]{2,1,0:T(8,128)(2,1)}, bf16[8,160,640]{2,1,0:T(8,128)(2,1)}, u32[]{:S(2)}, u32[]{:S(2)}) collective-permute-start(bf16[8,160,640]{2,1,0:T(8,128)(2,1)} %get-tuple-element.28.refs_1_.packed), channel_id=1, source_target_pairs={{0,2},{2,0},{4,6},{6,4},{8,10},{10,8},{12,14},{14,12},{16,18},{18,... | collective-permute-start | bytes 4915208 | tf_op jit(solution)/shard_map/ppermute | solution.py:249
  63.7 45.9 %collective-permute-start.9 = (bf16[8,160,640]{2,1,0:T(8,128)(2,1)}, bf16[8,160,640]{2,1,0:T(8,128)(2,1)}, u32[]{:S(2)}, u32[]{:S(2)}) collective-permute-start(bf16[8,160,640]{2,1,0:T(8,128)(2,1)} %get-tuple-element.29.refs_0_), channel_id=1, source_target_pairs={{0,2},{2,0},{4,6},{6,4},{8,10},{10,8},{12,14},{14,12},{16,18},{18,... | collective-permute-start | bytes 4915208 | tf_op jit(solution)/shard_map/ppermute | solution.py:249
  64.7 41.4 %collective-permute-start = (bf16[512,1280]{1,0:T(8,128)(2,1)S(1)}, bf16[512,1280]{1,0:T(8,128)(2,1)}, u32[]{:S(2)}, u32[]{:S(2)}) collective-permute-start(bf16[512,1280]{1,0:T(8,128)(2,1)S(1)} %fusion.4.n_own), channel_id=1, source_target_pairs={{0,1},{1,0},{2,3},{3,2},{4,5},{5,4},{6,7},{7,6},{8,9},{9,8},{10,11... | collective-permute-start | bytes 3932168 | tf_op jit(solution)/shard_map/ppermute | solution.py:252
  68.4 24.4 %collective-permute-start.27 = (bf16[3,160,512]{2,1,0:T(8,128)(2,1)}, bf16[3,160,512]{2,1,0:T(8,128)(2,1)}, u32[]{:S(2)}, u32[]{:S(2)}) collective-permute-start(bf16[3,160,512]{2,1,0:T(8,128)(2,1)} %get-tuple-element.27), channel_id=1, source_target_pairs={{0,16},{2,18},{4,20},{6,22},{8,24},{10,26},{12,28},{14,30},{16,0},... | collective-permute-start | bytes 1474568 | tf_op jit(solution)/shard_map/ppermute | solution.py:249
  70.8 24.8 %collective-permute-start.26 = (bf16[3,160,512]{2,1,0:T(8,128)(2,1)}, bf16[3,160,512]{2,1,0:T(8,128)(2,1)S(1)}, u32[]{:S(2)}, u32[]{:S(2)}) collective-permute-start(bf16[3,160,512]{2,1,0:T(8,128)(2,1)} %get-tuple-element.27), channel_id=1, source_target_pairs={{0,8},{2,10},{4,12},{6,14},{8,0},{10,2},{12,4},{14,6},{16,24},{18,... | collective-permute-start | bytes 1474568 | tf_op jit(solution)/shard_map/ppermute | solution.py:249
  95.6 33.6 %collective-permute-start.16 = (bf16[3,160,768]{2,1,0:T(8,128)(2,1)S(1)}, bf16[3,160,768]{2,1,0:T(8,128)(2,1)S(1)}, u32[]{:S(2)}, u32[]{:S(2)}) collective-permute-start(bf16[3,160,768]{2,1,0:T(8,128)(2,1)S(1)} %get-tuple-element.23), channel_id=1, source_target_pairs={{0,16},{2,18},{4,20},{6,22},{8,24},{10,26},{12,28},{14,30},{16,0},... | collective-permute-start | bytes 2211848 | tf_op jit(solution)/shard_map/ppermute | solution.py:249
  106.1 35.1 %collective-permute-start.15 = (bf16[3,160,768]{2,1,0:T(8,128)(2,1)S(1)}, bf16[3,160,768]{2,1,0:T(8,128)(2,1)S(1)}, u32[]{:S(2)}, u32[]{:S(2)}) collective-permute-start(bf16[3,160,768]{2,1,0:T(8,128)(2,1)S(1)} %get-tuple-element.23), channel_id=1, source_target_pairs={{0,8},{2,10},{4,12},{6,14},{8,0},{10,2},{12,4},{14,6},{16,24},{18,... | collective-permute-start | bytes 2211848 | tf_op jit(solution)/shard_map/ppermute | solution.py:249
  106.1 36.5 %collective-permute-start.18 = (bf16[3,160,768]{2,1,0:T(8,128)(2,1)S(1)}, bf16[3,160,768]{2,1,0:T(8,128)(2,1)S(1)}, u32[]{:S(2)}, u32[]{:S(2)}) collective-permute-start(bf16[3,160,768]{2,1,0:T(8,128)(2,1)S(1)} %get-tuple-element.23), channel_id=1, source_target_pairs={{0,4},{2,6},{4,0},{6,2},{8,12},{10,14},{12,8},{14,10},{16,20},{18,... | collective-permute-start | bytes 2211848 | tf_op jit(solution)/shard_map/ppermute | solution.py:249
  107.6 44.1 %collective-permute-start.28 = (bf16[3,160,512]{2,1,0:T(8,128)(2,1)}, bf16[3,160,512]{2,1,0:T(8,128)(2,1)S(1)}, u32[]{:S(2)}, u32[]{:S(2)}) collective-permute-start(bf16[3,160,512]{2,1,0:T(8,128)(2,1)} %collective-permute-done.27), channel_id=1, source_target_pairs={{0,8},{2,10},{4,12},{6,14},{8,0},{10,2},{12,4},{14,6},{16,24},{18,... | collective-permute-start | bytes 1474568 | tf_op jit(solution)/shard_map/ppermute | solution.py:249
  109.6 56.0 %collective-permute-start.12 = (bf16[8,160,640]{2,1,0:T(8,128)(2,1)}, bf16[8,160,640]{2,1,0:T(8,128)(2,1)S(1)}, u32[]{:S(2)}, u32[]{:S(2)}) collective-permute-start(bf16[8,160,640]{2,1,0:T(8,128)(2,1)} %get-tuple-element.28.refs_1_.packed), channel_id=1, source_target_pairs={{2,3},{3,2},{6,7},{7,6},{10,11},{11,10},{14,15},{15,14},{18,19},{1... | collective-permute-start | bytes 4915208 | tf_op jit(solution)/shard_map/ppermute | solution.py:328
  129.2 34.1 %collective-permute-start.30 = (bf16[3,160,512]{2,1,0:T(8,128)(2,1)}, bf16[3,160,512]{2,1,0:T(8,128)(2,1)S(1)}, u32[]{:S(2)}, u32[]{:S(2)}) collective-permute-start(bf16[3,160,512]{2,1,0:T(8,128)(2,1)} %collective-permute-done.27), channel_id=1, source_target_pairs={{0,4},{2,6},{4,0},{6,2},{8,12},{10,14},{12,8},{14,10},{16,20},{18,... | collective-permute-start | bytes 1474568 | tf_op jit(solution)/shard_map/ppermute | solution.py:249
  141.2 22.7 %collective-permute-start.31 = (bf16[3,160,512]{2,1,0:T(8,128)(2,1)S(1)}, bf16[3,160,512]{2,1,0:T(8,128)(2,1)S(1)}, u32[]{:S(2)}, u32[]{:S(2)}) collective-permute-start(bf16[3,160,512]{2,1,0:T(8,128)(2,1)S(1)} %collective-permute-done.26), channel_id=1, source_target_pairs={{0,4},{2,6},{4,0},{6,2},{8,12},{10,14},{12,8},{14,10},{16,20},{18,... | collective-permute-start | bytes 1474568 | tf_op jit(solution)/shard_map/ppermute | solution.py:249
  142.7 23.0 %collective-permute-start.17 = (bf16[3,160,768]{2,1,0:T(8,128)(2,1)S(1)}, bf16[3,160,768]{2,1,0:T(8,128)(2,1)S(1)}, u32[]{:S(2)}, u32[]{:S(2)}) collective-permute-start(bf16[3,160,768]{2,1,0:T(8,128)(2,1)S(1)} %collective-permute-done.16), channel_id=1, source_target_pairs={{0,8},{2,10},{4,12},{6,14},{8,0},{10,2},{12,4},{14,6},{16,24},{18,... | collective-permute-start | bytes 2211848 | tf_op jit(solution)/shard_map/ppermute | solution.py:249
  151.7 29.0 %collective-permute-start.19 = (bf16[3,160,768]{2,1,0:T(8,128)(2,1)S(1)}, bf16[3,160,768]{2,1,0:T(8,128)(2,1)}, u32[]{:S(2)}, u32[]{:S(2)}) collective-permute-start(bf16[3,160,768]{2,1,0:T(8,128)(2,1)S(1)} %collective-permute-done.16), channel_id=1, source_target_pairs={{0,4},{2,6},{4,0},{6,2},{8,12},{10,14},{12,8},{14,10},{16,20},{18,... | collective-permute-start | bytes 2211848 | tf_op jit(solution)/shard_map/ppermute | solution.py:249
  165.6 25.8 %collective-permute-start.13 = (bf16[8,160,640]{2,1,0:T(8,128)(2,1)S(1)}, bf16[8,160,640]{2,1,0:T(8,128)(2,1)S(1)}, u32[]{:S(2)}, u32[]{:S(2)}) collective-permute-start(bf16[8,160,640]{2,1,0:T(8,128)(2,1)S(1)} %collective-permute-done.12.y_own), channel_id=1, source_target_pairs={{2,0},{6,4},{10,8},{14,12},{18,16},{22,20},{26,24},{30,28},{3,1},{... | collective-permute-start | bytes 4915208 | tf_op jit(solution)/shard_map/ppermute | solution.py:331
  179.4 21.5 %collective-permute-start.20 = (bf16[3,160,768]{2,1,0:T(8,128)(2,1)S(1)}, bf16[3,160,768]{2,1,0:T(8,128)(2,1)S(1)}, u32[]{:S(2)}, u32[]{:S(2)}) collective-permute-start(bf16[3,160,768]{2,1,0:T(8,128)(2,1)S(1)} %collective-permute-done.15), channel_id=1, source_target_pairs={{0,4},{2,6},{4,0},{6,2},{8,12},{10,14},{12,8},{14,10},{16,20},{18,... | collective-permute-start | bytes 2211848 | tf_op jit(solution)/shard_map/ppermute | solution.py:249
  180.7 40.8 %collective-permute-start.33 = (bf16[4,3,160,512]{3,2,1,0:T(8,128)(2,1)S(1)}, bf16[4,3,160,512]{3,2,1,0:T(8,128)(2,1)}, u32[]{:S(2)}, u32[]{:S(2)}) collective-permute-start(bf16[4,3,160,512]{3,2,1,0:T(8,128)(2,1)S(1)} %pad_maximum_fusion.1.refs_0_), channel_id=1, source_target_pairs={{0,2},{2,0},{4,6},{6,4},{8,10},{10,8},{12,14},{14,12},{16,18},{18,... | collective-permute-start | bytes 5898248 | tf_op jit(solution)/shard_map/ppermute | solution.py:249
  180.7 20.6 %collective-permute-start.34 = (bf16[2,3,160,512]{3,2,1,0:T(8,128)(2,1)S(1)}, bf16[2,3,160,512]{3,2,1,0:T(8,128)(2,1)S(1)}, u32[]{:S(2)}, u32[]{:S(2)}) collective-permute-start(bf16[2,3,160,512]{3,2,1,0:T(8,128)(2,1)S(1)} %pad_maximum_fusion.4.refs_1_), channel_id=1, source_target_pairs={{0,2},{2,0},{4,6},{6,4},{8,10},{10,8},{12,14},{14,12},{16,18},{18,... | collective-permute-start | bytes 2949128 | tf_op jit(solution)/shard_map/ppermute | solution.py:249
  181.3 62.5 %collective-permute-start.22 = (bf16[4,3,160,768]{3,2,1,0:T(8,128)(2,1)}, bf16[4,3,160,768]{3,2,1,0:T(8,128)(2,1)}, u32[]{:S(2)}, u32[]{:S(2)}) collective-permute-start(bf16[4,3,160,768]{3,2,1,0:T(8,128)(2,1)} %pad_maximum_fusion.refs_0_), channel_id=1, source_target_pairs={{0,2},{2,0},{4,6},{6,4},{8,10},{10,8},{12,14},{14,12},{16,18},{18,... | collective-permute-start | bytes 8847368 | tf_op jit(solution)/shard_map/ppermute | solution.py:249
  200.9 35.3 %collective-permute-start.37 = (bf16[512,1280]{1,0:T(8,128)(2,1)}, bf16[512,1280]{1,0:T(8,128)(2,1)}, u32[]{:S(2)}, u32[]{:S(2)}) collective-permute-start(bf16[512,1280]{1,0:T(8,128)(2,1)} %get-tuple-element.13.x_ref), channel_id=1, source_target_pairs={{0,1},{1,0},{2,3},{3,2},{4,5},{5,4},{6,7},{7,6},{8,9},{9,8},{10,11... | collective-permute-start | bytes 3932168 | tf_op jit(solution)/shard_map/ppermute | solution.py:252
  202.7 18.8 %collective-permute-start.21 = (bf16[3,160,768]{2,1,0:T(8,128)(2,1)}, bf16[3,160,768]{2,1,0:T(8,128)(2,1)}, u32[]{:S(2)}, u32[]{:S(2)}) collective-permute-start(bf16[3,160,768]{2,1,0:T(8,128)(2,1)} %collective-permute-done.19), channel_id=1, source_target_pairs={{0,8},{2,10},{4,12},{6,14},{8,0},{10,2},{12,4},{14,6},{16,24},{18,... | collective-permute-start | bytes 2211848 | tf_op jit(solution)/shard_map/ppermute | solution.py:249
  205.9 37.8 %collective-permute-start.23 = (bf16[2,3,160,768]{3,2,1,0:T(8,128)(2,1)}, bf16[2,3,160,768]{3,2,1,0:T(8,128)(2,1)}, u32[]{:S(2)}, u32[]{:S(2)}) collective-permute-start(bf16[2,3,160,768]{3,2,1,0:T(8,128)(2,1)} %pad_maximum_fusion.2.refs_1_), channel_id=1, source_target_pairs={{0,2},{2,0},{4,6},{6,4},{8,10},{10,8},{12,14},{14,12},{16,18},{18,... | collective-permute-start | bytes 4423688 | tf_op jit(solution)/shard_map/ppermute | solution.py:249
  221.5 22.2 %collective-permute-start.24 = (bf16[3,160,768]{2,1,0:T(8,128)(2,1)}, bf16[3,160,768]{2,1,0:T(8,128)(2,1)S(1)}, u32[]{:S(2)}, u32[]{:S(2)}) collective-permute-start(bf16[3,160,768]{2,1,0:T(8,128)(2,1)} %copy-done.7), channel_id=1, source_target_pairs={{0,2},{2,0},{4,6},{6,4},{8,10},{10,8},{12,14},{14,12},{16,18},{18,... | collective-permute-start | bytes 2211848 | tf_op jit(solution)/shard_map/ppermute | solution.py:249
  221.5 22.2 %collective-permute-start.25 = (bf16[3,160,768]{2,1,0:T(8,128)(2,1)}, bf16[3,160,768]{2,1,0:T(8,128)(2,1)S(1)}, u32[]{:S(2)}, u32[]{:S(2)}) collective-permute-start(bf16[3,160,768]{2,1,0:T(8,128)(2,1)} %collective-permute-done.21), channel_id=1, source_target_pairs={{0,2},{2,0},{4,6},{6,4},{8,10},{10,8},{12,14},{14,12},{16,18},{18,... | collective-permute-start | bytes 2211848 | tf_op jit(solution)/shard_map/ppermute | solution.py:249
  255.0 30.7 %collective-permute-start.38 = (bf16[512,1280]{1,0:T(8,128)(2,1)S(1)}, bf16[512,1280]{1,0:T(8,128)(2,1)S(1)}, u32[]{:S(2)}, u32[]{:S(2)}) collective-permute-start(bf16[512,1280]{1,0:T(8,128)(2,1)S(1)} %shard_map.138), channel_id=1, source_target_pairs={{0,1},{1,0},{2,3},{3,2},{4,5},{5,4},{6,7},{7,6},{8,9},{9,8},{10,11... | collective-permute-start | bytes 3932168 | tf_op jit(solution)/shard_map/ppermute | solution.py:252
  (43 other events, 277.7 us)

commit v3 on v2

--- a/solution.py
+++ b/solution.py
@@ -184,7 +184,7 @@
         n2_ref[sl, :] = layer_norm(r, gain[...])
 
 
-def ff_body(has_acc, groups, lines, place, x_ref, *refs):
+def ff_body(has_acc, first_row, groups, lines, place, x_ref, *refs):
     half = len(groups)
     stacks, rest = (refs[:half], refs[half : 2 * half]), refs[2 * half :]
     acc_in = None
@@ -192,6 +192,7 @@
         acc_in, rest = rest[0], rest[1:]
     *outs, w, sems = rest
     acc = outs.pop() if len(outs) == 2 else outs[0]
+    taken = slice(first_row, first_row + acc.shape[0])
     rows = refs[0].shape[2]
     sub = w.shape[-1]
     n_sub = refs[0].shape[-1] // sub
@@ -208,14 +209,14 @@
         each(0, s, lambda cp: cp.start())
 
     def product(slot):
-        x = x_ref[...]
+        x = x_ref[taken, :]
         gate = dot(x, w[slot, 0])
         value = dot(x, w[slot, 1])
         hidden = (0.5 * gate * (1.0 + lax.erf(gate * (0.5**0.5))) * value).astype(BF16)
         return dot_nt(hidden, w[slot, 2])
 
     if has_acc:
-        acc[...] = acc_in[...]
+        acc[...] = acc_in[taken, :]
     else:
         acc[...] = jnp.zeros_like(acc)
     for c_flip in range(CORES):
@@ -339,16 +340,15 @@
     )(place, gain_row, noised, mixed_own, m_recv, packed0, second0, y_own, y_partner)
     n2_peer = flip_y(n2)
 
-    def ff(tokens, groups, stacks, hc, sub, acc, out_dtype):
+    def ff(tokens, first_row, t, groups, stacks, hc, sub, acc, out_dtype):
         n_sub = hc // sub
-        t = tokens.shape[0]
         args = [place, tokens, *stacks]
         specs = [smem_spec(), vmem_spec()] + [hbm_spec()] * len(stacks)
         if acc is not None:
             args.append(acc)
             specs.append(vmem_spec())
         return call(
-            functools.partial(ff_body, acc is not None, groups, lines),
+            functools.partial(ff_body, acc is not None, first_row, groups, lines),
             [jax.ShapeDtypeStruct((t, width), out_dtype)],
             specs,
             ([pltpu.VMEM((t, width), F32)] if out_dtype != F32 else [])
@@ -378,10 +378,17 @@
                 stacks.append((piece[None], flip(piece, CORE)[None]))
         stacks = [pair[n] for n in range(2) for pair in stacks]
         last = index == len(chunks) - 1
-        peer_acc = ff(n2_peer, groups, stacks, hc, sub, peer_acc, BF16 if last else F32)
-        own_acc = ff(n2, groups, stacks, hc, sub, own_acc, F32)
+        if last:
+            half = rows // 2
+            parts = [
+                ff(n2_peer, n * half, half, groups, stacks, hc, sub, peer_acc, BF16)
+                for n in range(2)
+            ]
+        else:
+            peer_acc = ff(n2_peer, 0, rows, groups, stacks, hc, sub, peer_acc, F32)
+        own_acc = ff(n2, 0, rows, groups, stacks, hc, sub, own_acc, F32)
         start += hc
-    recv = flip_y(peer_acc)
+    recv = jnp.concatenate([flip_y(part) for part in parts])
 
     ratio = sigma[0] / alpha[0]
     base = noised.astype(F32) / alpha[0] - ratio * (resid.astype(F32) + own_acc)

time: 308 us -> 362 us (1.18)
  starting transfers between devices: 39.9 us -> 60.9 us
  waiting for transfers between devices: 147 us -> 168 us
  Pallas kernels: 74.9 us -> 81.4 us
    ppermute x5 -> x6, waiting for transfers between devices: 19 us -> 47.8 us  [flip_y(): return lax.ppermute(value, 'mp', [(0, 1), (1, 0)])]
    ppermute x38, starting transfers between devices: 32.3 us -> 48 us  [flip(): return lax.ppermute(value, 'dp', [(i, i ^ bits) for i in range(dp)])]
    ppermute x38, waiting for transfers between devices: 126 us -> 119 us  [flip(): return lax.ppermute(value, 'dp', [(i, i ^ bits) for i in range(dp)])]
    pallas_call x4 -> x5, Pallas kernels: 37.3 us -> 43.6 us  [ff(): call(functools.partial(ff_body, acc is not None, first_row, groups, lines...]
    unnamed x64 -> x90, local copies, waits for them, and re-layouts: 15.3 us -> 18.5 us
  transfers between devices with their start and end apart: 46 -> 47, of which waited for: 19 -> 19; matrix products, arithmetic and copies ran while one was open for 8% -> 7% of each run, Pallas kernels for 21% -> 18%
where the time goes in v3:
time: 362 us; the launch traced here: 361 us
  waiting for transfers between devices  168 us (46%)
  Pallas kernels  81.4 us (22%)
  starting transfers between devices  60.9 us (17%)
  other arithmetic  24.5 us (7%)
  local copies, waits for them, and re-layouts  20.7 us (6%)
  between operations  5.01 us (1%)
    ppermute x38, waiting for transfers between devices, flip(): return lax.ppermute(value, 'dp', [(i, i ^ bits) for i in range(dp)])  119 us
    ppermute x38, starting transfers between devices, flip(): return lax.ppermute(value, 'dp', [(i, i ^ bits) for i in range(dp)])  48 us
    ppermute x6, waiting for transfers between devices, flip_y(): return lax.ppermute(value, 'mp', [(0, 1), (1, 0)])  47.8 us
    pallas_call x5, Pallas kernels, ff(): call(functools.partial(ff_body, acc is not None, first_row, groups, lines...  43.6 us
    pallas_call x2, Pallas kernels, attend(): call(attn_body, [half_shape], [vmem_spec()] * 3, [], 12 * 10 ** 9, 8 * ro...  20.2 us
    unnamed x90, local copies, waits for them, and re-layouts  18.5 us
    pallas_call x1, Pallas kernels, fast_shards(): call(functools.partial(qkv_body, scale, lines), [half_shape, half_shape,...  9.87 us
    another operation x6, other arithmetic, swap_packed(): packed = jnp.stack(parts)  9.17 us
  transfers between devices with their start and end apart: 47, of which 19 were waited for; matrix products, arithmetic and copies ran while one was open for 7% of the time, Pallas kernels for 18%

profile of v3, /device:TPU:0, one launch (start us, length us, event | category | flops | bytes accessed | tf_op | source)
XLA Modules:
  0.0 360.6 jit_solution(1260309778791994660)
XLA Ops:
  8.7 2.5 convert_reduce_fusion
  13.1 3.1 collective-permute-start.2
  16.2 2.6 collective-permute-start.3
  23.7 2.6 collective-permute-start.27
  26.3 38.2 %collective-permute-done.3 = bf16[2,160,640]{2,1,0:T(8,128)(2,1)S(1)} collective-permute-done((bf16[2,160,640]{2,1,0:T(8,128)(2,1)S(1)}, bf16[2,160,640]{2,1,0:T(8,128)(2,1)S(1)}, u32[]{:S(2)}, u32[]{:S(2)}) %collective-permute-start.3) | collective-permute-done | bytes 409632 | tf_op jit(solution)/shard_map/ppermute | solution.py:250
  67.6 30.8 %collective-permute-done.4 = bf16[2,160,640]{2,1,0:T(8,128)(2,1)S(1)} collective-permute-done((bf16[2,160,640]{2,1,0:T(8,128)(2,1)S(1)}, bf16[2,160,640]{2,1,0:T(8,128)(2,1)S(1)}, u32[]{:S(2)}, u32[]{:S(2)}) %collective-permute-start.4) | collective-permute-done | bytes 409632 | tf_op jit(solution)/shard_map/ppermute | solution.py:250
  101.9 4.3 %collective-permute-done.7 = bf16[2,160,640]{2,1,0:T(8,128)(2,1)S(1)} collective-permute-done((bf16[2,160,640]{2,1,0:T(8,128)(2,1)S(1)}, bf16[2,160,640]{2,1,0:T(8,128)(2,1)S(1)}, u32[]{:S(2)}, u32[]{:S(2)}) %collective-permute-start.7) | collective-permute-done | bytes 409632 | tf_op jit(solution)/shard_map/ppermute | solution.py:250
  110.0 6.0 %collective-permute-done.8 = bf16[2,160,640]{2,1,0:T(8,128)(2,1)S(1)} collective-permute-done((bf16[2,160,640]{2,1,0:T(8,128)(2,1)S(1)}, bf16[2,160,640]{2,1,0:T(8,128)(2,1)S(1)}, u32[]{:S(2)}, u32[]{:S(2)}) %collective-permute-start.8) | collective-permute-done | bytes 409632 | tf_op jit(solution)/shard_map/ppermute | solution.py:250
  119.5 8.8 %collective-permute-done.15 = bf16[3,160,768]{2,1,0:T(8,128)(2,1)S(1)} collective-permute-done((bf16[3,160,768]{2,1,0:T(8,128)(2,1)}, bf16[3,160,768]{2,1,0:T(8,128)(2,1)S(1)}, u32[]{:S(2)}, u32[]{:S(2)}) %collective-permute-start.15) | collective-permute-done | bytes 737312 | tf_op jit(solution)/shard_map/ppermute | solution.py:250
  129.8 1.9 collective-permute-start.12
  131.7 4.5 %collective-permute-done.17 = bf16[3,160,768]{2,1,0:T(8,128)(2,1)S(1)} collective-permute-done((bf16[3,160,768]{2,1,0:T(8,128)(2,1)S(1)}, bf16[3,160,768]{2,1,0:T(8,128)(2,1)S(1)}, u32[]{:S(2)}, u32[]{:S(2)}) %collective-permute-start.17) | collective-permute-done | bytes 737312 | tf_op jit(solution)/shard_map/ppermute | solution.py:250
  139.0 2.1 pad_maximum_fusion.refs_0_
  141.1 19.1 %collective-permute-done.n_peer = bf16[512,1280]{1,0:T(8,128)(2,1)} collective-permute-done((bf16[512,1280]{1,0:T(8,128)(2,1)}, bf16[512,1280]{1,0:T(8,128)(2,1)}, u32[]{:S(2)}, u32[]{:S(2)}) %collective-permute-start) | collective-permute-done | bytes 1310752 | tf_op jit(solution)/shard_map/ppermute | solution.py:253
  163.8 9.9 %shard_map.131 = (bf16[5,512,128]{2,1,0:T(8,128)(2,1)S(1)}, bf16[5,512,128]{2,1,0:T(8,128)(2,1)S(1)}, bf16[5,1024,128]{2,1,0:T(8,128)(2,1)S(1)}, bf16[5,1024,128]{2,1,0:T(8,128)(2,1)S(1)}) custom-call(s32[4]{0:T(128)S(1)} %pad_add_fusion.place, bf16[512,1280]{1,0:T(8,128)(2,1)} %fusion.4.n_own, bf16[512,1280]{1,0:T(8,128)(2,1)} %collective-permute-done.n_peer, ...), custom_call_target="tpu_custom_call" | custom-call | flops 8000000000 | bytes 11796480 | tf_op jit(solution)/shard_map/pallas_call | solution.py:308
  175.7 11.6 %collective-permute-done.19 = bf16[3,160,768]{2,1,0:T(8,128)(2,1)S(1)} collective-permute-done((bf16[3,160,768]{2,1,0:T(8,128)(2,1)S(1)}, bf16[3,160,768]{2,1,0:T(8,128)(2,1)S(1)}, u32[]{:S(2)}, u32[]{:S(2)}) %collective-permute-start.19) | collective-permute-done | bytes 737312 | tf_op jit(solution)/shard_map/ppermute | solution.py:250
  187.3 8.0 %collective-permute-done.20 = bf16[3,160,768]{2,1,0:T(8,128)(2,1)} collective-permute-done((bf16[3,160,768]{2,1,0:T(8,128)(2,1)S(1)}, bf16[3,160,768]{2,1,0:T(8,128)(2,1)}, u32[]{:S(2)}, u32[]{:S(2)}) %collective-permute-start.20) | collective-permute-done | bytes 737312 | tf_op jit(solution)/shard_map/ppermute | solution.py:250
  196.8 10.1 %shard_map.133 = bf16[5,512,128]{2,1,0:T(8,128)(2,1)S(1)} custom-call(bf16[5,512,128]{2,1,0:T(8,128)(2,1)S(1)} %get-tuple-element.11.q_ref, bf16[5,1024,128]{2,1,0:T(8,128)(2,1)S(1)} %get-tuple-element.9.k_ref, bf16[5,1024,128]{2,1,0:T(8,128)(2,1)S(1)} %get-tuple-element.10.v_ref), custom_call_target="tpu_custom_call" | custom-call | flops 12000000000 | bytes 5242880 | tf_op jit(solution)/shard_map/pallas_call | solution.py:321
  211.1 2.4 pad_maximum_fusion.2.refs_1_
  215.0 9.4 %collective-permute-done.11.m_peer = bf16[5,512,128]{2,1,0:T(8,128)(2,1)S(1)} collective-permute-done((bf16[5,512,128]{2,1,0:T(8,128)(2,1)S(1)}, bf16[5,512,128]{2,1,0:T(8,128)(2,1)S(1)}, u32[]{:S(2)}, u32[]{:S(2)}) %collective-permute-start.11) | collective-permute-done | bytes 655392 | tf_op jit(solution)/shard_map/ppermute | solution.py:253
  224.6 10.1 %shard_map.132.m_own = bf16[5,512,128]{2,1,0:T(8,128)(2,1)S(1)} custom-call(bf16[5,512,128]{2,1,0:T(8,128)(2,1)S(1)} %get-tuple-element.8.q_ref, bf16[5,1024,128]{2,1,0:T(8,128)(2,1)S(1)} %get-tuple-element.9.k_ref, bf16[5,1024,128]{2,1,0:T(8,128)(2,1)S(1)} %get-tuple-element.10.v_ref), custom_call_target="tpu_custom_call" | custom-call | flops 12000000000 | bytes 5242880 | tf_op jit(solution)/shard_map/pallas_call | solution.py:321
  234.7 7.8 %shard_map.134 = (bf16[512,1280]{1,0:T(8,128)(2,1)S(1)}, bf16[512,1280]{1,0:T(8,128)(2,1)}) custom-call(s32[4]{0:T(128)S(1)} %pad_add_fusion.place, f32[1,1280]{1,0:T(1,128)S(1)} %reshape.41.gain, bf16[512,1280]{1,0:T(8,128)(2,1)S(1)} %copy-done.1, bf16[5,512,128]{2,1,0:T(8,128)(2,1)S(1)} %shard_map.132.m_own, ...), custom_call_target="tpu_custom_call" | custom-call | flops 4000000000 | bytes 6553600 | tf_op jit(solution)/shard_map/pallas_call | solution.py:333
  257.5 7.8 %shard_map.135.refs_8_ = f32[512,1280]{1,0:T(8,128)S(1)} custom-call(s32[4]{0:T(128)S(1)} %pad_add_fusion.place, bf16[512,1280]{1,0:T(8,128)(2,1)} %get-tuple-element.13.x_ref, bf16[4,3,160,512]{3,2,1,0:T(8,128)(2,1)S(1)} %copy-done.4, bf16[2,3,160,512]{3,2,1,0:T(8,128)(2,1)S(1)} %copy-done.9, bf16[1,3,160,512]{3,2,1,0:T(8,128)(2,1)S(1)} %bitcast.46, ...), custom_call_target="tpu_custom_call" | custom-call | flops 4026531840 | bytes 7864320 | tf_op jit(solution)/shard_map/pallas_call | solution.py:350
  265.4 11.7 %shard_map.136 = f32[512,1280]{1,0:T(8,128)S(1)} custom-call(s32[4]{0:T(128)S(1)} %pad_add_fusion.place, bf16[512,1280]{1,0:T(8,128)(2,1)} %get-tuple-element.13.x_ref, bf16[4,3,160,768]{3,2,1,0:T(8,128)(2,1)S(1)} %pad_maximum_fusion.refs_0_, bf16[2,3,160,768]{3,2,1,0:T(8,128)(2,1)} %pad_maximum_fusion.2.refs_1_, bf16[1,3,160,768]{3,2,1,0:T(8,128)(2,1)} %bitcast.18.refs_2_, ...), custom_call_target="tpu_custom_call" | custom-call | flops 6039797760 | bytes 11796480 | tf_op jit(solution)/shard_map/pallas_call | solution.py:350
  277.3 7.6 %shard_map.137.refs_8_ = f32[512,1280]{1,0:T(8,128)S(1)} custom-call(s32[4]{0:T(128)S(1)} %pad_add_fusion.place, bf16[512,1280]{1,0:T(8,128)(2,1)} %collective-permute-done.37.x_ref, bf16[4,3,160,512]{3,2,1,0:T(8,128)(2,1)S(1)} %copy-done.5, bf16[2,3,160,512]{3,2,1,0:T(8,128)(2,1)S(1)} %copy-done.10, bf16[1,3,160,512]{3,2,1,0:T(8,128)(2,1)S(1)} %bitcast.47, ...), custom_call_target="tpu_custom_call" | custom-call | flops 4026531840 | bytes 7864320 | tf_op jit(solution)/shard_map/pallas_call | solution.py:350
  284.8 8.0 %shard_map.139 = bf16[256,1280]{1,0:T(8,128)(2,1)S(1)} custom-call(s32[4]{0:T(128)S(1)} %pad_add_fusion.place, bf16[512,1280]{1,0:T(8,128)(2,1)} %collective-permute-done.37.x_ref, bf16[4,3,160,768]{3,2,1,0:T(8,128)(2,1)S(1)} %pad_maximum_fusion.refs_0_, bf16[2,3,160,768]{3,2,1,0:T(8,128)(2,1)} %pad_maximum_fusion.2.refs_1_, ...), custom_call_target="tpu_custom_call" | custom-call | flops 3019898880 | bytes 11796480 | tf_op jit(solution)/shard_map/pallas_call | solution.py:350
  293.5 8.5 %shard_map.138 = bf16[256,1280]{1,0:T(8,128)(2,1)S(1)} custom-call(s32[4]{0:T(128)S(1)} %pad_add_fusion.place, bf16[512,1280]{1,0:T(8,128)(2,1)} %collective-permute-done.37.x_ref, bf16[4,3,160,768]{3,2,1,0:T(8,128)(2,1)S(1)} %pad_maximum_fusion.refs_0_, bf16[2,3,160,768]{3,2,1,0:T(8,128)(2,1)} %pad_maximum_fusion.2.refs_1_, ...), custom_call_target="tpu_custom_call" | custom-call | flops 3019898880 | bytes 11796480 | tf_op jit(solution)/shard_map/pallas_call | solution.py:350
  304.5 6.1 %collective-permute-done.39 = bf16[256,1280]{1,0:T(8,128)(2,1)S(1)} collective-permute-done((bf16[256,1280]{1,0:T(8,128)(2,1)S(1)}, bf16[256,1280]{1,0:T(8,128)(2,1)S(1)}, u32[]{:S(2)}, u32[]{:S(2)}) %collective-permute-start.39) | collective-permute-done | bytes 655392 | tf_op jit(solution)/shard_map/ppermute | solution.py:253
  310.6 13.1 %collective-permute-done.38 = bf16[256,1280]{1,0:T(8,128)(2,1)S(1)} collective-permute-done((bf16[256,1280]{1,0:T(8,128)(2,1)S(1)}, bf16[256,1280]{1,0:T(8,128)(2,1)S(1)}, u32[]{:S(2)}, u32[]{:S(2)}) %collective-permute-start.38) | collective-permute-done | bytes 655392 | tf_op jit(solution)/shard_map/ppermute | solution.py:253
  323.6 2.7 fusion.8
  329.4 2.4 collective-permute-start.43
  335.5 20.1 %collective-permute-start.46 = (f32[8,128]{1,0:T(8,128)S(1)}, f32[8,128]{1,0:T(8,128)S(1)}, u32[]{:S(2)}, u32[]{:S(2)}) collective-permute-start(f32[8,128]{1,0:T(8,128)S(1)} %add_add_fusion.1), channel_id=1, source_target_pairs={{0,24},{2,26},{4,28},{6,30},{8,16},{10,18},{12,20},{14,22},{16,8},... | collective-permute-start | bytes 12296 | tf_op jit(solution)/shard_map/ppermute | solution.py:250
  357.2 2.9 collective-permute-done.45
  (192 shorter events, 69.0 us)
Async XLA Ops:
  13.1 51.4 %collective-permute-start.2 = (bf16[2,160,640]{2,1,0:T(8,128)(2,1)S(1)}, bf16[2,160,640]{2,1,0:T(8,128)(2,1)S(1)}, u32[]{:S(2)}, u32[]{:S(2)}) collective-permute-start(bf16[2,160,640]{2,1,0:T(8,128)(2,1)S(1)} %pad_maximum_fusion.7), channel_id=1, source_target_pairs={{0,8},{2,10},{4,12},{6,14},{8,0},{10,2},{12,4},{14,6},{16,24},{18,... | collective-permute-start | bytes 1228808 | tf_op jit(solution)/shard_map/ppermute | solution.py:250
  16.2 48.3 %collective-permute-start.3 = (bf16[2,160,640]{2,1,0:T(8,128)(2,1)S(1)}, bf16[2,160,640]{2,1,0:T(8,128)(2,1)S(1)}, u32[]{:S(2)}, u32[]{:S(2)}) collective-permute-start(bf16[2,160,640]{2,1,0:T(8,128)(2,1)S(1)} %pad_maximum_fusion.7), channel_id=1, source_target_pairs={{0,16},{2,18},{4,20},{6,22},{8,24},{10,26},{12,28},{14,30},{16,0},... | collective-permute-start | bytes 1228808 | tf_op jit(solution)/shard_map/ppermute | solution.py:250
  18.7 81.9 %collective-permute-start.5 = (bf16[2,160,640]{2,1,0:T(8,128)(2,1)S(1)}, bf16[2,160,640]{2,1,0:T(8,128)(2,1)S(1)}, u32[]{:S(2)}, u32[]{:S(2)}) collective-permute-start(bf16[2,160,640]{2,1,0:T(8,128)(2,1)S(1)} %pad_maximum_fusion.7), channel_id=1, source_target_pairs={{0,4},{2,6},{4,0},{6,2},{8,12},{10,14},{12,8},{14,10},{16,20},{18,... | collective-permute-start | bytes 1228808 | tf_op jit(solution)/shard_map/ppermute | solution.py:250
  22.4 87.0 %collective-permute-start.16 = (bf16[3,160,768]{2,1,0:T(8,128)(2,1)}, bf16[3,160,768]{2,1,0:T(8,128)(2,1)S(1)}, u32[]{:S(2)}, u32[]{:S(2)}) collective-permute-start(bf16[3,160,768]{2,1,0:T(8,128)(2,1)} %get-tuple-element.23), channel_id=1, source_target_pairs={{0,16},{2,18},{4,20},{6,22},{8,24},{10,26},{12,28},{14,30},{16,0},... | collective-permute-start | bytes 2211848 | tf_op jit(solution)/shard_map/ppermute | solution.py:250
  23.7 85.6 %collective-permute-start.27 = (bf16[3,160,512]{2,1,0:T(8,128)(2,1)S(1)}, bf16[3,160,512]{2,1,0:T(8,128)(2,1)}, u32[]{:S(2)}, u32[]{:S(2)}) collective-permute-start(bf16[3,160,512]{2,1,0:T(8,128)(2,1)S(1)} %get-tuple-element.27), channel_id=1, source_target_pairs={{0,16},{2,18},{4,20},{6,22},{8,24},{10,26},{12,28},{14,30},{16,0},... | collective-permute-start | bytes 1474568 | tf_op jit(solution)/shard_map/ppermute | solution.py:250
  64.5 33.8 %collective-permute-start.4 = (bf16[2,160,640]{2,1,0:T(8,128)(2,1)S(1)}, bf16[2,160,640]{2,1,0:T(8,128)(2,1)S(1)}, u32[]{:S(2)}, u32[]{:S(2)}) collective-permute-start(bf16[2,160,640]{2,1,0:T(8,128)(2,1)S(1)} %collective-permute-done.3), channel_id=1, source_target_pairs={{0,8},{2,10},{4,12},{6,14},{8,0},{10,2},{12,4},{14,6},{16,24},{18,... | collective-permute-start | bytes 1228808 | tf_op jit(solution)/shard_map/ppermute | solution.py:250
  64.5 36.9 %collective-permute-start.6 = (bf16[2,160,640]{2,1,0:T(8,128)(2,1)S(1)}, bf16[2,160,640]{2,1,0:T(8,128)(2,1)S(1)}, u32[]{:S(2)}, u32[]{:S(2)}) collective-permute-start(bf16[2,160,640]{2,1,0:T(8,128)(2,1)S(1)} %collective-permute-done.2), channel_id=1, source_target_pairs={{0,4},{2,6},{4,0},{6,2},{8,12},{10,14},{12,8},{14,10},{16,20},{18,... | collective-permute-start | bytes 1228808 | tf_op jit(solution)/shard_map/ppermute | solution.py:250
  109.4 18.9 %collective-permute-start.15 = (bf16[3,160,768]{2,1,0:T(8,128)(2,1)}, bf16[3,160,768]{2,1,0:T(8,128)(2,1)S(1)}, u32[]{:S(2)}, u32[]{:S(2)}) collective-permute-start(bf16[3,160,768]{2,1,0:T(8,128)(2,1)} %get-tuple-element.23), channel_id=1, source_target_pairs={{0,8},{2,10},{4,12},{6,14},{8,0},{10,2},{12,4},{14,6},{16,24},{18,... | collective-permute-start | bytes 2211848 | tf_op jit(solution)/shard_map/ppermute | solution.py:250
  109.4 20.4 %collective-permute-start.30 = (bf16[3,160,512]{2,1,0:T(8,128)(2,1)}, bf16[3,160,512]{2,1,0:T(8,128)(2,1)S(1)}, u32[]{:S(2)}, u32[]{:S(2)}) collective-permute-start(bf16[3,160,512]{2,1,0:T(8,128)(2,1)} %collective-permute-done.27), channel_id=1, source_target_pairs={{0,4},{2,6},{4,0},{6,2},{8,12},{10,14},{12,8},{14,10},{16,20},{18,... | collective-permute-start | bytes 1474568 | tf_op jit(solution)/shard_map/ppermute | solution.py:250
  115.9 20.2 %collective-permute-start.17 = (bf16[3,160,768]{2,1,0:T(8,128)(2,1)S(1)}, bf16[3,160,768]{2,1,0:T(8,128)(2,1)S(1)}, u32[]{:S(2)}, u32[]{:S(2)}) collective-permute-start(bf16[3,160,768]{2,1,0:T(8,128)(2,1)S(1)} %collective-permute-done.16), channel_id=1, source_target_pairs={{0,8},{2,10},{4,12},{6,14},{8,0},{10,2},{12,4},{14,6},{16,24},{18,... | collective-permute-start | bytes 2211848 | tf_op jit(solution)/shard_map/ppermute | solution.py:250
  117.5 44.3 %collective-permute-start.9 = (bf16[8,160,640]{2,1,0:T(8,128)(2,1)}, bf16[8,160,640]{2,1,0:T(8,128)(2,1)}, u32[]{:S(2)}, u32[]{:S(2)}) collective-permute-start(bf16[8,160,640]{2,1,0:T(8,128)(2,1)} %get-tuple-element.29.refs_0_), channel_id=1, source_target_pairs={{0,2},{2,0},{4,6},{6,4},{8,10},{10,8},{12,14},{14,12},{16,18},{18,... | collective-permute-start | bytes 4915208 | tf_op jit(solution)/shard_map/ppermute | solution.py:250
  117.5 44.8 %collective-permute-start.10 = (bf16[8,160,640]{2,1,0:T(8,128)(2,1)}, bf16[8,160,640]{2,1,0:T(8,128)(2,1)}, u32[]{:S(2)}, u32[]{:S(2)}) collective-permute-start(bf16[8,160,640]{2,1,0:T(8,128)(2,1)} %get-tuple-element.28.refs_1_.packed), channel_id=1, source_target_pairs={{0,2},{2,0},{4,6},{6,4},{8,10},{10,8},{12,14},{14,12},{16,18},{18,... | collective-permute-start | bytes 4915208 | tf_op jit(solution)/shard_map/ppermute | solution.py:250
  128.3 32.0 %collective-permute-start = (bf16[512,1280]{1,0:T(8,128)(2,1)}, bf16[512,1280]{1,0:T(8,128)(2,1)}, u32[]{:S(2)}, u32[]{:S(2)}) collective-permute-start(bf16[512,1280]{1,0:T(8,128)(2,1)} %fusion.4.n_own), channel_id=1, source_target_pairs={{0,1},{1,0},{2,3},{3,2},{4,5},{5,4},{6,7},{7,6},{8,9},{9,8},{10,11... | collective-permute-start | bytes 3932168 | tf_op jit(solution)/shard_map/ppermute | solution.py:253
  129.8 65.6 %collective-permute-start.12 = (bf16[8,160,640]{2,1,0:T(8,128)(2,1)}, bf16[8,160,640]{2,1,0:T(8,128)(2,1)}, u32[]{:S(2)}, u32[]{:S(2)}) collective-permute-start(bf16[8,160,640]{2,1,0:T(8,128)(2,1)} %get-tuple-element.28.refs_1_.packed), channel_id=1, source_target_pairs={{2,3},{3,2},{6,7},{7,6},{10,11},{11,10},{14,15},{15,14},{18,19},{1... | collective-permute-start | bytes 4915208 | tf_op jit(solution)/shard_map/ppermute | solution.py:329
  136.2 24.1 %collective-permute-start.18 = (bf16[3,160,768]{2,1,0:T(8,128)(2,1)}, bf16[3,160,768]{2,1,0:T(8,128)(2,1)}, u32[]{:S(2)}, u32[]{:S(2)}) collective-permute-start(bf16[3,160,768]{2,1,0:T(8,128)(2,1)} %get-tuple-element.23), channel_id=1, source_target_pairs={{0,4},{2,6},{4,0},{6,2},{8,12},{10,14},{12,8},{14,10},{16,20},{18,... | collective-permute-start | bytes 2211848 | tf_op jit(solution)/shard_map/ppermute | solution.py:250
  161.7 25.6 %collective-permute-start.19 = (bf16[3,160,768]{2,1,0:T(8,128)(2,1)S(1)}, bf16[3,160,768]{2,1,0:T(8,128)(2,1)S(1)}, u32[]{:S(2)}, u32[]{:S(2)}) collective-permute-start(bf16[3,160,768]{2,1,0:T(8,128)(2,1)S(1)} %copy-done.33), channel_id=1, source_target_pairs={{0,4},{2,6},{4,0},{6,2},{8,12},{10,14},{12,8},{14,10},{16,20},{18,... | collective-permute-start | bytes 2211848 | tf_op jit(solution)/shard_map/ppermute | solution.py:250
  162.3 33.1 %collective-permute-start.20 = (bf16[3,160,768]{2,1,0:T(8,128)(2,1)S(1)}, bf16[3,160,768]{2,1,0:T(8,128)(2,1)}, u32[]{:S(2)}, u32[]{:S(2)}) collective-permute-start(bf16[3,160,768]{2,1,0:T(8,128)(2,1)S(1)} %copy-done.35), channel_id=1, source_target_pairs={{0,4},{2,6},{4,0},{6,2},{8,12},{10,14},{12,8},{14,10},{16,20},{18,... | collective-permute-start | bytes 2211848 | tf_op jit(solution)/shard_map/ppermute | solution.py:250
  173.7 39.8 %collective-permute-start.34 = (bf16[2,3,160,512]{3,2,1,0:T(8,128)(2,1)S(1)}, bf16[2,3,160,512]{3,2,1,0:T(8,128)(2,1)S(1)}, u32[]{:S(2)}, u32[]{:S(2)}) collective-permute-start(bf16[2,3,160,512]{3,2,1,0:T(8,128)(2,1)S(1)} %pad_maximum_fusion.5.refs_1_), channel_id=1, source_target_pairs={{0,2},{2,0},{4,6},{6,4},{8,10},{10,8},{12,14},{14,12},{16,18},{18,... | collective-permute-start | bytes 2949128 | tf_op jit(solution)/shard_map/ppermute | solution.py:250
  174.2 32.8 %collective-permute-start.32 = (bf16[3,160,512]{2,1,0:T(8,128)(2,1)S(1)}, bf16[3,160,512]{2,1,0:T(8,128)(2,1)S(1)}, u32[]{:S(2)}, u32[]{:S(2)}) collective-permute-start(bf16[3,160,512]{2,1,0:T(8,128)(2,1)S(1)} %collective-permute-done.28), channel_id=1, source_target_pairs={{0,4},{2,6},{4,0},{6,2},{8,12},{10,14},{12,8},{14,10},{16,20},{18,... | collective-permute-start | bytes 1474568 | tf_op jit(solution)/shard_map/ppermute | solution.py:250
  187.3 22.7 %collective-permute-start.35 = (bf16[3,160,512]{2,1,0:T(8,128)(2,1)S(1)}, bf16[3,160,512]{2,1,0:T(8,128)(2,1)S(1)}, u32[]{:S(2)}, u32[]{:S(2)}) collective-permute-start(bf16[3,160,512]{2,1,0:T(8,128)(2,1)S(1)} %collective-permute-done.31), channel_id=1, source_target_pairs={{0,2},{2,0},{4,6},{6,4},{8,10},{10,8},{12,14},{14,12},{16,18},{18,... | collective-permute-start | bytes 1474568 | tf_op jit(solution)/shard_map/ppermute | solution.py:250
  195.4 70.0 %collective-permute-start.22 = (bf16[4,3,160,768]{3,2,1,0:T(8,128)(2,1)S(1)}, bf16[4,3,160,768]{3,2,1,0:T(8,128)(2,1)}, u32[]{:S(2)}, u32[]{:S(2)}) collective-permute-start(bf16[4,3,160,768]{3,2,1,0:T(8,128)(2,1)S(1)} %pad_maximum_fusion.refs_0_), channel_id=1, source_target_pairs={{0,2},{2,0},{4,6},{6,4},{8,10},{10,8},{12,14},{14,12},{16,18},{18,... | collective-permute-start | bytes 8847368 | tf_op jit(solution)/shard_map/ppermute | solution.py:250
  195.4 29.0 %collective-permute-start.13 = (bf16[8,160,640]{2,1,0:T(8,128)(2,1)}, bf16[8,160,640]{2,1,0:T(8,128)(2,1)S(1)}, u32[]{:S(2)}, u32[]{:S(2)}) collective-permute-start(bf16[8,160,640]{2,1,0:T(8,128)(2,1)} %collective-permute-done.12.y_own), channel_id=1, source_target_pairs={{2,0},{6,4},{10,8},{14,12},{18,16},{22,20},{26,24},{30,28},{3,1},{... | collective-permute-start | bytes 4915208 | tf_op jit(solution)/shard_map/ppermute | solution.py:332
  210.0 35.8 %collective-permute-start.33 = (bf16[4,3,160,512]{3,2,1,0:T(8,128)(2,1)S(1)}, bf16[4,3,160,512]{3,2,1,0:T(8,128)(2,1)S(1)}, u32[]{:S(2)}, u32[]{:S(2)}) collective-permute-start(bf16[4,3,160,512]{3,2,1,0:T(8,128)(2,1)S(1)} %pad_maximum_fusion.1.refs_0_), channel_id=1, source_target_pairs={{0,2},{2,0},{4,6},{6,4},{8,10},{10,8},{12,14},{14,12},{16,18},{18,... | collective-permute-start | bytes 5898248 | tf_op jit(solution)/shard_map/ppermute | solution.py:250
  214.4 50.9 %collective-permute-start.23 = (bf16[2,3,160,768]{3,2,1,0:T(8,128)(2,1)}, bf16[2,3,160,768]{3,2,1,0:T(8,128)(2,1)}, u32[]{:S(2)}, u32[]{:S(2)}) collective-permute-start(bf16[2,3,160,768]{3,2,1,0:T(8,128)(2,1)} %pad_maximum_fusion.2.refs_1_), channel_id=1, source_target_pairs={{0,2},{2,0},{4,6},{6,4},{8,10},{10,8},{12,14},{14,12},{16,18},{18,... | collective-permute-start | bytes 4423688 | tf_op jit(solution)/shard_map/ppermute | solution.py:250
  224.4 21.5 %collective-permute-start.21 = (bf16[3,160,768]{2,1,0:T(8,128)(2,1)S(1)}, bf16[3,160,768]{2,1,0:T(8,128)(2,1)}, u32[]{:S(2)}, u32[]{:S(2)}) collective-permute-start(bf16[3,160,768]{2,1,0:T(8,128)(2,1)S(1)} %collective-permute-done.19), channel_id=1, source_target_pairs={{0,8},{2,10},{4,12},{6,14},{8,0},{10,2},{12,4},{14,6},{16,24},{18,... | collective-permute-start | bytes 2211848 | tf_op jit(solution)/shard_map/ppermute | solution.py:250
  224.4 19.2 %collective-permute-start.36 = (bf16[3,160,512]{2,1,0:T(8,128)(2,1)S(1)}, bf16[3,160,512]{2,1,0:T(8,128)(2,1)S(1)}, u32[]{:S(2)}, u32[]{:S(2)}) collective-permute-start(bf16[3,160,512]{2,1,0:T(8,128)(2,1)S(1)} %collective-permute-done.32), channel_id=1, source_target_pairs={{0,2},{2,0},{4,6},{6,4},{8,10},{10,8},{12,14},{14,12},{16,18},{18,... | collective-permute-start | bytes 1474568 | tf_op jit(solution)/shard_map/ppermute | solution.py:250
  244.3 32.8 %collective-permute-start.37 = (bf16[512,1280]{1,0:T(8,128)(2,1)}, bf16[512,1280]{1,0:T(8,128)(2,1)}, u32[]{:S(2)}, u32[]{:S(2)}) collective-permute-start(bf16[512,1280]{1,0:T(8,128)(2,1)} %get-tuple-element.13.x_ref), channel_id=1, source_target_pairs={{0,1},{1,0},{2,3},{3,2},{4,5},{5,4},{6,7},{7,6},{8,9},{9,8},{10,11... | collective-permute-start | bytes 3932168 | tf_op jit(solution)/shard_map/ppermute | solution.py:253
  245.9 19.5 %collective-permute-start.24 = (bf16[3,160,768]{2,1,0:T(8,128)(2,1)}, bf16[3,160,768]{2,1,0:T(8,128)(2,1)}, u32[]{:S(2)}, u32[]{:S(2)}) collective-permute-start(bf16[3,160,768]{2,1,0:T(8,128)(2,1)} %collective-permute-done.20), channel_id=1, source_target_pairs={{0,2},{2,0},{4,6},{6,4},{8,10},{10,8},{12,14},{14,12},{16,18},{18,... | collective-permute-start | bytes 2211848 | tf_op jit(solution)/shard_map/ppermute | solution.py:250
  247.2 18.2 %collective-permute-start.25 = (bf16[3,160,768]{2,1,0:T(8,128)(2,1)}, bf16[3,160,768]{2,1,0:T(8,128)(2,1)}, u32[]{:S(2)}, u32[]{:S(2)}) collective-permute-start(bf16[3,160,768]{2,1,0:T(8,128)(2,1)} %collective-permute-done.21), channel_id=1, source_target_pairs={{0,2},{2,0},{4,6},{6,4},{8,10},{10,8},{12,14},{14,12},{16,18},{18,... | collective-permute-start | bytes 2211848 | tf_op jit(solution)/shard_map/ppermute | solution.py:250
  292.9 17.7 %collective-permute-start.39 = (bf16[256,1280]{1,0:T(8,128)(2,1)S(1)}, bf16[256,1280]{1,0:T(8,128)(2,1)S(1)}, u32[]{:S(2)}, u32[]{:S(2)}) collective-permute-start(bf16[256,1280]{1,0:T(8,128)(2,1)S(1)} %shard_map.139), channel_id=1, source_target_pairs={{0,1},{1,0},{2,3},{3,2},{4,5},{5,4},{6,7},{7,6},{8,9},{9,8},{10,11... | collective-permute-start | bytes 1966088 | tf_op jit(solution)/shard_map/ppermute | solution.py:253
  301.9 21.7 %collective-permute-start.38 = (bf16[256,1280]{1,0:T(8,128)(2,1)S(1)}, bf16[256,1280]{1,0:T(8,128)(2,1)S(1)}, u32[]{:S(2)}, u32[]{:S(2)}) collective-permute-start(bf16[256,1280]{1,0:T(8,128)(2,1)S(1)} %shard_map.138), channel_id=1, source_target_pairs={{0,1},{1,0},{2,3},{3,2},{4,5},{5,4},{6,7},{7,6},{8,9},{9,8},{10,11... | collective-permute-start | bytes 1966088 | tf_op jit(solution)/shard_map/ppermute | solution.py:253
  335.5 21.7 %collective-permute-start.46 = (f32[8,128]{1,0:T(8,128)S(1)}, f32[8,128]{1,0:T(8,128)S(1)}, u32[]{:S(2)}, u32[]{:S(2)}) collective-permute-start(f32[8,128]{1,0:T(8,128)S(1)} %add_add_fusion.1), channel_id=1, source_target_pairs={{0,24},{2,26},{4,28},{6,30},{8,16},{10,18},{12,20},{14,22},{16,8},... | collective-permute-start | bytes 12296 | tf_op jit(solution)/shard_map/ppermute | solution.py:250
  (57 other events, 608.8 us)
